TPU v7x, 32 devices: a whole 2x2x4 slice. The times are simulated.
32 devices in a mesh: win: 8 (over z, x), fsdp: 4 (over y, core).
Axes of the slice: x: 2, y: 2, z: 4, core: 2. Of those that a mesh axis runs over, the one named last changes fastest.
Arguments:
- queries: bfloat16 [8192, 2560], P(('win', 'fsdp')), may hold values from -5 to 5
- keys: bfloat16 [8192, 2560], P(('win', 'fsdp')), may hold values from -5 to 5
- values: bfloat16 [8192, 2560], P(('win', 'fsdp')), may hold values from -6 to 6
- stream: bfloat16 [8192, 5120], P(('win', 'fsdp')), may hold values from -0.59765625 to 0.59765625
- out_weight: bfloat16 [2560, 5120], P('fsdp', 'win'), may hold values from -0.125 to 0.125
- gate: float32 [5120], replicated, may hold values from 0.5 to 2
- head_shift: float32 [5120], replicated, may hold values from -3 to 3
- head_scale: float32 [5120], replicated, may hold values from 0.25 to 1.75
- head_weight: bfloat16 [5120, 64], replicated, may hold values from -0.078125 to 0.078125
- latents: float32 [128, 4096], P('win', 'fsdp'), may hold values from -6 to 6
- step_size: float32 [1], replicated, may hold values from 0.5 to 1
- intersections: int32 [8], replicated, may hold values from 1 to 4
- ramps: int32 [8, 4, 2], replicated, may hold values from 1 to 16
Outputs:
- blended: float32 [128, 4096], P('win', 'fsdp')
All inputs are finite; a program needn't handle non-finite values.
Results may differ from a plain program's by a relative error of at most 0.0065.
Values may be sent and summed in bfloat16 or wider, within the bound.
A program may use at most 128 MiB of HBM per device.

v0:
```python
import functools
import math

import jax
import jax.numpy as jnp
from jax import lax
from jax.experimental import pallas as pl
from jax.experimental.pallas import tpu as pltpu
from jax.sharding import PartitionSpec as P

HEADS = 20
HD = 128
FD = 4
EPSILON = 0.001
MESH = pl.DeviceIdType.MESH
F32 = jnp.float32
BF16 = jnp.bfloat16


def kernel(
    ring, n_blk, q_ref, k_ref, v_ref, stream_ref, ow_ref, gate_ref, shift_ref, scale_ref, wt_ref,
    lat_ref, step_ref, inter_ref, ramps_ref, out_ref,
    qkv, attended, weights, residual, side_out, side_in, own_out, own_in, cross_hold, cross_out,
    cross_in, hidden, flat, fresh, before, after, head_rows,
    qkv_send, qkv_recv, qkv_local, w_send, w_recv, w_local, res_sem, side_send, side_recv,
    own_send, own_recv, cross_send, cross_recv, edge_send, edge_recv,
):
    win, n_win = lax.axis_index("win"), lax.axis_size("win")
    me, groups = lax.axis_index("fsdp"), lax.axis_size("fsdp")
    rows = q_ref.shape[0]
    heads = qkv.shape[1]
    width = weights.shape[2]
    chip, core = me // 2, me % 2
    sibling = chip * 2 + (1 - core)
    far_chip = 1 - chip
    far = far_chip * 2 + core
    far_sibling = far_chip * 2 + (1 - core)
    inputs = (q_ref, k_ref, v_ref)

    up_win, down_win = lax.rem(win + 1, n_win), lax.rem(win + n_win - 1, n_win)
    half_ring = n_win // 2

    def spot_of(w):
        odd = w % 2
        return (1 - odd) * (w // 2) + odd * (n_win - 1 - w // 2)

    def win_of(spot):
        late = spot // half_ring
        return (1 - late) * (2 * spot) + late * (2 * (n_win - 1 - spot) + 1)

    spot = spot_of(win)
    ring_next = win_of(lax.rem(spot + 1, n_win))
    ring_prev = win_of(lax.rem(spot + n_win - 1, n_win))

    if ring:
        blocks = [win]
        for s in range(1, half_ring):
            blocks.append(win_of(lax.rem(spot - s + n_win, n_win)))
            blocks.append(win_of(lax.rem(spot + s, n_win)))
        blocks.append(win_of(lax.rem(spot + half_ring, n_win)))
    else:
        blocks = [jnp.int32(j) for j in range(n_blk)]

    def columns(j):
        return pl.ds(pl.multiple_of(blocks[j] * width, 128), width)

    def qkv_copy(t, h, to, slot):
        return pltpu.make_async_remote_copy(
            src_ref=inputs[t].at[:, pl.ds(pl.multiple_of((to * heads + h) * HD, HD), HD)],
            dst_ref=qkv.at[t, h, pl.ds(pl.multiple_of(me * rows, rows), rows), :],
            send_sem=qkv_send.at[t, h, slot],
            recv_sem=qkv_recv.at[t, h, me],
            device_id={"fsdp": to},
            device_id_type=MESH,
        )

    def qkv_arrival(t, h, source):
        return pltpu.make_async_remote_copy(
            src_ref=inputs[t].at[:, pl.ds(pl.multiple_of((source * heads + h) * HD, HD), HD)],
            dst_ref=qkv.at[t, h, pl.ds(pl.multiple_of(source * rows, rows), rows), :],
            send_sem=qkv_send.at[t, h, 0],
            recv_sem=qkv_recv.at[t, h, source],
            device_id={"fsdp": source},
            device_id_type=MESH,
        )

    def qkv_own(t, h):
        return pltpu.make_async_copy(
            inputs[t].at[:, pl.ds(pl.multiple_of((me * heads + h) * HD, HD), HD)],
            qkv.at[t, h, pl.ds(pl.multiple_of(me * rows, rows), rows), :],
            qkv_local.at[t, h],
        )

    peers = (far, far_sibling, sibling)

    def weight_copy(src, dst, slot, to):
        return pltpu.make_async_remote_copy(
            src_ref=src, dst_ref=dst, send_sem=w_send.at[slot], recv_sem=w_recv.at[slot],
            device_id={"win": to}, device_id_type=MESH,
        )

    depth_half = weights.shape[1] // 2
    last = n_blk - 1

    def forward_copies(s):
        if s < half_ring:
            up_src = ow_ref if s == 1 else weights.at[2 * s - 3]
            down_src = ow_ref if s == 1 else weights.at[2 * s - 2]
            return (
                weight_copy(up_src, weights.at[2 * s - 1], 2 * s - 2, ring_next),
                weight_copy(down_src, weights.at[2 * s], 2 * s - 1, ring_prev),
            )
        top, low = pl.ds(0, depth_half), pl.ds(depth_half, depth_half)
        return (
            weight_copy(weights.at[2 * s - 3, top], weights.at[last, top], 2 * s - 2, ring_next),
            weight_copy(weights.at[2 * s - 2, low], weights.at[last, low], 2 * s - 1, ring_prev),
        )

    def weight_local(j):
        source = ow_ref if ring else ow_ref.at[:, columns(j)]
        return pltpu.make_async_copy(source, weights.at[j], w_local.at[j])

    def residual_copy(j):
        return pltpu.make_async_copy(
            stream_ref.at[:, columns(j)], residual.at[j], res_sem.at[j]
        )

    barrier = pltpu.get_barrier_semaphore()
    for peer in peers:
        pl.semaphore_signal(barrier, inc=1, device_id={"fsdp": peer}, device_id_type=MESH)
    greeted = [up_win, down_win] + ([ring_next, ring_prev] if ring else [])
    for other in greeted:
        pl.semaphore_signal(barrier, inc=1, device_id={"win": other}, device_id_type=MESH)
    pl.semaphore_wait(barrier, len(peers) + len(greeted))

    def start_heads(kinds):
        def start_head(h, carry):
            for t in kinds:
                for slot, peer in enumerate(peers):
                    qkv_copy(t, h, peer, slot).start()
                qkv_own(t, h).start()
            return carry

        lax.fori_loop(0, heads, start_head, 0)

    start_heads((1, 2))
    if ring:
        for copy in forward_copies(1):
            copy.start()
    start_heads((0,))
    for j in range(1 if ring else n_blk):
        weight_local(j).start()
    for j in range(n_blk):
        residual_copy(j).start()

    head = wt_ref[...].astype(F32)
    for i, vector in enumerate((scale_ref, shift_ref)):
        head_rows[8 * i : 8 * i + 8] = lax.dot_general(
            jnp.broadcast_to(vector[...], (8, head.shape[1])), head, (((1,), (1,)), ((), ())),
            precision=lax.Precision.HIGHEST, preferred_element_type=F32,
        )

    factor = math.log2(math.e) / math.sqrt(HD)

    def attend(h, first):
        def piece(i, carry):
            at = pl.ds(pl.multiple_of(first + i * rows, rows), rows)
            query = qkv[0, h, at, :]
            scores = lax.dot_general(
                query, qkv[1, h], (((1,), (1,)), ((), ())), preferred_element_type=F32
            )
            highest = jnp.max(scores, axis=-1, keepdims=True)
            exponent = jnp.exp2((scores - highest) * factor)
            denominator = jnp.sum(exponent, axis=-1, keepdims=True)
            summed = jnp.dot(exponent.astype(BF16), qkv[2, h], preferred_element_type=F32)
            attended[at, pl.ds(pl.multiple_of(h * HD, HD), HD)] = (summed / denominator).astype(
                BF16
            )
            return carry

        lax.fori_loop(0, 2, piece, 0)

    def near_head(h, carry):
        for t in (1, 2):
            for source in peers:
                qkv_arrival(t, h, source).wait_recv()
            qkv_own(t, h).wait()
        qkv_arrival(0, h, sibling).wait_recv()
        qkv_own(0, h).wait()
        attend(h, chip * 2 * rows)
        return carry

    lax.fori_loop(0, heads, near_head, 0)
    if ring:
        for copy in forward_copies(1):
            copy.wait_recv()
        for copy in forward_copies(2):
            copy.start()

    def far_head(h, carry):
        for source in (far, far_sibling):
            qkv_arrival(0, h, source).wait_recv()
        attend(h, far_chip * 2 * rows)
        return carry

    lax.fori_loop(0, heads, far_head, 0)

    def part_copy(src, dst, send, recv, j, to):
        return pltpu.make_async_remote_copy(
            src_ref=src.at[j], dst_ref=dst.at[j], send_sem=send.at[j], recv_sem=recv.at[j],
            device_id={"fsdp": to}, device_id_type=MESH,
        )

    def side_copy(j):
        return part_copy(side_out, side_in, side_send, side_recv, j, sibling)

    def own_copy(j):
        return part_copy(own_out, own_in, own_send, own_recv, j, sibling)

    def cross_copy(j):
        return part_copy(cross_out, cross_in, cross_send, cross_recv, j, far)

    def product(group, j):
        at = pl.ds(pl.multiple_of(group * rows, rows), rows)
        return jnp.dot(attended[at, :], weights[j], preferred_element_type=F32)

    for j in range(n_blk):
        if not ring or j == 0:
            weight_local(j).wait()
        elif j % 2 == 1:
            s = (j + 1) // 2
            if s > 1:
                for copy in forward_copies(s):
                    copy.wait_recv()
                if s < half_ring:
                    for copy in forward_copies(s + 1):
                        copy.start()
        side_out[j] = product(far_sibling, j).astype(BF16)
        side_copy(j).start()
        cross_hold[...] = product(far, j)
        own_out[j] = product(sibling, j).astype(BF16)
        own_copy(j).start()
        hidden[j] = product(me, j)
        side_copy(j).wait_recv()
        cross_out[j] = (cross_hold[...] + side_in[j].astype(F32)).astype(BF16)
        cross_copy(j).start()
        residual_copy(j).wait()
        own_copy(j).wait_recv()
        hidden[j] = residual[j].astype(F32) + gate_ref[:, columns(j)] * (
            hidden[j] + own_in[j].astype(F32)
        )

    centres, spreads, raw, pivot = [], [], None, None
    for j in range(n_blk):
        cross_copy(j).wait_recv()
        block = hidden[j] + gate_ref[:, columns(j)] * cross_in[j].astype(F32)
        if j == 0:
            pivot = jnp.sum(block, axis=-1, keepdims=True) * (1.0 / width)
        shifted = block - pivot
        term = lax.dot_general(
            (shifted * scale_ref[:, columns(j)]).astype(BF16), wt_ref[:, columns(j)],
            (((1,), (1,)), ((), ())), preferred_element_type=F32,
        )
        raw = term if raw is None else raw + term
        centre = jnp.sum(shifted, axis=-1, keepdims=True) * (1.0 / width)
        centred = shifted - centre
        centres.append(centre)
        spreads.append(jnp.sum(centred * centred, axis=-1, keepdims=True))
    mean = functools.reduce(jnp.add, centres) * (1.0 / n_blk)
    spread = functools.reduce(jnp.add, spreads)
    for centre in centres:
        spread = spread + width * (centre - mean) * (centre - mean)
    inverse = 1.0 / jnp.sqrt(spread * (1.0 / (width * n_blk)) + EPSILON)
    velocity = inverse * (raw - mean * head_rows[:1]) + head_rows[8:9]

    channels = wt_ref.shape[0]
    frames, wide = lat_ref.shape
    per_frame = wide // channels
    flat[:, :channels] = velocity
    step = step_ref[0]
    for p in range(0, per_frame, 2):
        pair = jnp.concatenate(
            [flat[pl.ds(p + i, frames, stride=per_frame), :][:, :channels] for i in range(2)],
            axis=1,
        )
        at = pl.ds(p * channels, 2 * channels)
        fresh[:, at] = lat_ref[:, at] + step * pair

    edge = before.shape[0]

    def edge_copy(src, dst, slot, to):
        return pltpu.make_async_remote_copy(
            src_ref=src, dst_ref=dst, send_sem=edge_send.at[slot], recv_sem=edge_recv.at[slot],
            device_id={"win": to}, device_id_type=MESH,
        )

    end_rows = pl.ds(frames - edge, edge)
    edges = (
        edge_copy(fresh.at[end_rows], before, 0, up_win),
        edge_copy(fresh.at[pl.ds(0, edge)], after, 1, down_win),
    )
    for copy in edges:
        copy.start()
    if frames > 2 * edge:
        middle = pl.ds(edge, frames - 2 * edge)
        out_ref[middle, :] = fresh[middle, :]
    index = lax.broadcasted_iota(jnp.int32, (edge, 1), 0)
    over_prev, over_next = inter_ref[down_win], inter_ref[win]
    zero = jnp.zeros((edge, 1), jnp.int32)

    def blend(aligned, mine, theirs_w, mine_w):
        theirs = theirs_w.astype(F32)
        own = jnp.where(mine_w > 0, mine_w, 1).astype(F32)
        return (theirs * aligned + own * mine) / (theirs + own)

    for copy in edges:
        copy.wait_recv()

    weight_theirs, weight_own = zero, zero
    for i in range(FD):
        hit = (index == i) & (index < over_prev)
        weight_theirs = jnp.where(hit, ramps_ref[2 * i, down_win], weight_theirs)
        weight_own = jnp.where(hit, ramps_ref[2 * i + 1, down_win], weight_own)
    aligned = jnp.zeros((edge, wide), F32)
    chosen = before[...]
    for o in range(1, FD + 1):
        hit = (zero + over_prev) == o
        aligned = jnp.where(hit, pltpu.roll(chosen, o, 0), aligned)
    out_ref[:edge, :] = blend(aligned, fresh[:edge, :], weight_theirs, weight_own)

    weight_theirs, weight_own = zero, zero
    for i in range(FD):
        hit = (index == edge - over_next + i)
        weight_own = jnp.where(hit, ramps_ref[2 * i, win], weight_own)
        weight_theirs = jnp.where(hit, ramps_ref[2 * i + 1, win], weight_theirs)
    aligned = jnp.zeros((edge, wide), F32)
    chosen = after[...]
    for o in range(1, FD + 1):
        hit = (zero + over_next) == o
        aligned = jnp.where(hit, pltpu.roll(chosen, edge - o, 0), aligned)
    out_ref[end_rows, :] = blend(aligned, fresh[end_rows, :], weight_theirs, weight_own)

    def finish_head(h, carry):
        for t in range(3):
            for slot, peer in enumerate(peers):
                qkv_copy(t, h, peer, slot).wait_send()
        return carry

    lax.fori_loop(0, heads, finish_head, 0)
    if ring:
        for s in range(1, half_ring + 1):
            for copy in forward_copies(s):
                copy.wait_send()
    for j in range(n_blk):
        side_copy(j).wait_send()
        own_copy(j).wait_send()
        cross_copy(j).wait_send()
    for copy in edges:
        copy.wait_send()


def local(
    queries,
    keys,
    values,
    stream,
    out_weight,
    gate,
    head_shift,
    head_scale,
    head_weight,
    latents,
    step_size,
    intersections,
    ramps,
):
    rows, features = queries.shape
    groups, n_win = lax.axis_size("fsdp"), lax.axis_size("win")
    heads = features // HD // groups
    depth, part = out_weight.shape
    model = stream.shape[1]
    ring = part % 128 == 0 and n_win % 2 == 0 and n_win >= 6
    if ring:
        n_blk, width = n_win, part
    else:
        n_blk = 8
        width = model // n_blk
        out_weight = lax.all_gather(out_weight, "win", axis=1, tiled=True)
    frames, wide = latents.shape
    edge = 8
    any_spec = pl.BlockSpec(memory_space=pl.ANY)
    vmem = pl.BlockSpec(memory_space=pltpu.VMEM)
    smem = pl.BlockSpec(memory_space=pltpu.SMEM)
    dma = pltpu.SemaphoreType.DMA
    parts = pltpu.VMEM((n_blk, rows, width), BF16)
    return pl.pallas_call(
        functools.partial(kernel, ring, n_blk),
        out_shape=jax.ShapeDtypeStruct(latents.shape, latents.dtype),
        in_specs=[any_spec] * 5 + [vmem] * 5 + [smem] * 3,
        out_specs=vmem,
        scratch_shapes=[
            pltpu.VMEM((3, heads, groups * rows, HD), BF16),
            pltpu.VMEM((groups * rows, heads * HD), BF16),
            pltpu.VMEM((n_blk, depth, width), BF16),
            parts, parts, parts, parts, parts,
            pltpu.VMEM((rows, width), F32),
            parts, parts,
            pltpu.VMEM((n_blk, rows, width), F32),
            pltpu.VMEM((rows, 128), F32),
            pltpu.VMEM((frames, wide), F32),
            pltpu.VMEM((edge, wide), F32),
            pltpu.VMEM((edge, wide), F32),
            pltpu.VMEM((16, head_weight.shape[1]), F32),
            dma((3, heads, 3)), dma((3, heads, groups)), dma((3, heads)),
            dma((n_blk,)), dma((n_blk,)), dma((n_blk,)), dma((n_blk,)),
            dma((n_blk,)), dma((n_blk,)), dma((n_blk,)), dma((n_blk,)),
            dma((n_blk,)), dma((n_blk,)), dma((2,)), dma((2,)),
        ],
        compiler_params=pltpu.CompilerParams(
            collective_id=0, has_side_effects=True, vmem_limit_bytes=60 * 1024 * 1024
        ),
    )(
        queries, keys, values, stream, out_weight,
        gate[None, :], head_shift[None, :], head_scale[None, :], head_weight.T, latents,
        step_size, intersections, jnp.transpose(ramps, (1, 2, 0)).reshape(-1, n_win),
    )


def solution(mesh):
    in_specs = (
        P(("win", "fsdp"), None),
        P(("win", "fsdp"), None),
        P(("win", "fsdp"), None),
        P(("win", "fsdp"), None),
        P("fsdp", "win"),
        P(),
        P(),
        P(),
        P(),
        P("win", "fsdp"),
        P(),
        P(),
        P(),
    )
    out_specs = P("win", "fsdp")
    return jax.shard_map(local, mesh=mesh, in_specs=in_specs, out_specs=out_specs, check_vma=False)
```

profile of v0, /device:TPU:0, one launch (start us, length us, event | category | flops | bytes accessed | tf_op | source)
XLA Modules:
  0.0 121.8 jit_solution(15383120598783172319)
XLA Ops:
  0.7 119.7 %shard_map.127 = f32[16,1024]{1,0:T(8,128)} custom-call(bf16[256,2560]{1,0:T(8,128)(2,1)} %q_ref.1, bf16[256,2560]{1,0:T(8,128)(2,1)} %k_ref.1, bf16[256,2560]{1,0:T(8,128)(2,1)} %v_ref.1, bf16[256,5120]{1,0:T(8,128)(2,1)} %stream_ref.1, bf16[640,640]{1,0:T(8,128)(2,1)} %ow_ref.1, f32[1,5120]{1,0:T(1,128)} %bitcast.8, f32[1,5120]{1,0:T(1,128)} %bitcast.9, ...), custom_call_target="tpu_custom_call" | custom-call | tf_op jit(solution)/shard_map/pallas_call | solution.py:396
  120.4 1.5 %copy.16 = f32[16,1024]{1,0:T(8,128)} copy(f32[16,1024]{1,0:T(8,128)} %shard_map.127) | data formatting | bytes 131072
where the time goes:
time: 122 us
  Pallas kernels  120 us (98%)
  local copies, waits for them, and re-layouts  1.47 us (1%)
    pallas_call x1, Pallas kernels, local(): pl.pallas_call(functools.partial(kernel, ring, n_blk), out_shape=jax.Shap...  120 us

commit v1 on v0

v1 whole, which is shorter than its diff:
```python
import functools
import math

import jax
import jax.numpy as jnp
from jax import lax
from jax.experimental import pallas as pl
from jax.experimental.pallas import tpu as pltpu
from jax.sharding import PartitionSpec as P

HEADS = 20
HD = 128
FD = 4
EPSILON = 0.001
MESH = pl.DeviceIdType.MESH
F32 = jnp.float32
BF16 = jnp.bfloat16


def kernel(
    ring, n_blk, q_ref, k_ref, v_ref, stream_ref, ow_ref, gate_hbm, shift_hbm, scale_hbm, wt_hbm,
    lat_hbm, step_ref, inter_ref, ramps_ref, out_ref,
    kv, queries, attended, weights, residual, far_hold, near_hold, side_out, side_in, own_out,
    own_in, cross_out, cross_in, hidden, flat, mine, before, after, head_rows,
    gate_ref, shift_ref, scale_ref, wt_ref, lat_ref,
    kv_send, kv_recv, kv_local, q_send, q_recv, q_local, w_send, w_recv, w_local, res_sem,
    par_sem, side_send, side_recv, own_send, own_recv, cross_send, cross_recv, edge_send,
    edge_recv,
):
    win, n_win = lax.axis_index("win"), lax.axis_size("win")
    me, groups = lax.axis_index("fsdp"), lax.axis_size("fsdp")
    rows = q_ref.shape[0]
    heads = kv.shape[1]
    width = weights.shape[2]
    frames, wide = lat_hbm.shape
    channels, model = wt_hbm.shape
    per_frame = rows // frames
    ends = FD * per_frame
    sizes = (2 * ends, rows - 2 * ends)
    pieces = (
        (0, 0, 0, ends),
        (0, rows - ends, ends, ends),
        (1, ends, 0, rows - 2 * ends),
    )
    chip, core = me // 2, me % 2
    sibling = chip * 2 + (1 - core)
    far_chip = 1 - chip
    far = far_chip * 2 + core
    far_sibling = far_chip * 2 + (1 - core)

    up_win, down_win = lax.rem(win + 1, n_win), lax.rem(win + n_win - 1, n_win)
    half_ring = n_win // 2

    def spot_of(w):
        odd = w % 2
        return (1 - odd) * (w // 2) + odd * (n_win - 1 - w // 2)

    def win_of(spot):
        late = spot // half_ring
        return (1 - late) * (2 * spot) + late * (2 * (n_win - 1 - spot) + 1)

    spot = spot_of(win)
    ring_next = win_of(lax.rem(spot + 1, n_win))
    ring_prev = win_of(lax.rem(spot + n_win - 1, n_win))

    if ring:
        blocks = [win]
        for s in range(1, half_ring):
            blocks.append(win_of(lax.rem(spot - s + n_win, n_win)))
            blocks.append(win_of(lax.rem(spot + s, n_win)))
        blocks.append(win_of(lax.rem(spot + half_ring, n_win)))
    else:
        blocks = [jnp.int32(j) for j in range(n_blk)]

    def columns(j):
        return pl.ds(pl.multiple_of(blocks[j] * width, 128), width)

    def head_columns(device, h):
        return pl.ds(pl.multiple_of((device * heads + h) * HD, HD), HD)

    def spots(device, size, start=0, length=None):
        length = size if length is None else length
        return pl.ds(pl.multiple_of(device * size + start, math.gcd(size, start)), length)

    peers = (far, far_sibling, sibling)
    pair = (k_ref, v_ref)

    def kv_copy(t, h, to, slot, source=None):
        source = me if source is None else source
        return pltpu.make_async_remote_copy(
            src_ref=pair[t].at[:, head_columns(to, h)],
            dst_ref=kv.at[t, h, spots(source, rows), :],
            send_sem=kv_send.at[t, h, slot],
            recv_sem=kv_recv.at[t, h, source],
            device_id={"fsdp": to},
            device_id_type=MESH,
        )

    def kv_own(t, h):
        return pltpu.make_async_copy(
            pair[t].at[:, head_columns(me, h)], kv.at[t, h, spots(me, rows), :], kv_local.at[t, h]
        )

    def q_copy(p, h, to, slot, source=None):
        chunk, first, start, length = pieces[p]
        source = me if source is None else source
        return pltpu.make_async_remote_copy(
            src_ref=q_ref.at[pl.ds(first, length), head_columns(to, h)],
            dst_ref=queries[chunk].at[h, spots(source, sizes[chunk], start, length), :],
            send_sem=q_send.at[p, h, slot],
            recv_sem=q_recv.at[p, h, source],
            device_id={"fsdp": to},
            device_id_type=MESH,
        )

    def q_own(p, h):
        chunk, first, start, length = pieces[p]
        return pltpu.make_async_copy(
            q_ref.at[pl.ds(first, length), head_columns(me, h)],
            queries[chunk].at[h, spots(me, sizes[chunk], start, length), :],
            q_local.at[p, h],
        )

    def weight_copy(src, dst, slot, to):
        return pltpu.make_async_remote_copy(
            src_ref=src, dst_ref=dst, send_sem=w_send.at[slot], recv_sem=w_recv.at[slot],
            device_id={"win": to}, device_id_type=MESH,
        )

    depth_half = weights.shape[1] // 2
    last = n_blk - 1

    def forward_copies(s):
        if s < half_ring:
            up_src = ow_ref if s == 1 else weights.at[2 * s - 3]
            down_src = ow_ref if s == 1 else weights.at[2 * s - 2]
            return (
                weight_copy(up_src, weights.at[2 * s - 1], 2 * s - 2, ring_next),
                weight_copy(down_src, weights.at[2 * s], 2 * s - 1, ring_prev),
            )
        top, low = pl.ds(0, depth_half), pl.ds(depth_half, depth_half)
        return (
            weight_copy(weights.at[2 * s - 3, top], weights.at[last, top], 2 * s - 2, ring_next),
            weight_copy(weights.at[2 * s - 2, low], weights.at[last, low], 2 * s - 1, ring_prev),
        )

    def weight_local(j):
        source = ow_ref if ring else ow_ref.at[:, columns(j)]
        return pltpu.make_async_copy(source, weights.at[j], w_local.at[j])

    def residual_copy(p):
        chunk, first, start, length = pieces[p]
        return pltpu.make_async_copy(
            stream_ref.at[pl.ds(first, length), :],
            residual[chunk].at[pl.ds(start, length), :],
            res_sem.at[p],
        )

    parameters = tuple(
        pltpu.make_async_copy(src, dst, par_sem.at[i])
        for i, (src, dst) in enumerate(
            (
                (scale_hbm, scale_ref),
                (shift_hbm, shift_ref),
                (wt_hbm, wt_ref),
                (gate_hbm, gate_ref),
                (lat_hbm, lat_ref),
            )
        )
    )

    barrier = pltpu.get_barrier_semaphore()
    for peer in peers:
        pl.semaphore_signal(barrier, inc=1, device_id={"fsdp": peer}, device_id_type=MESH)
    greeted = [up_win, down_win] + ([ring_next, ring_prev] if ring else [])
    for other in greeted:
        pl.semaphore_signal(barrier, inc=1, device_id={"win": other}, device_id_type=MESH)
    pl.semaphore_wait(barrier, len(peers) + len(greeted))

    def start_kv(h, carry):
        for t in range(2):
            for slot, peer in enumerate(peers):
                kv_copy(t, h, peer, slot).start()
            kv_own(t, h).start()
        return carry

    def start_q(h, carry, chosen):
        for p in chosen:
            for slot, peer in enumerate(peers):
                q_copy(p, h, peer, slot).start()
            q_own(p, h).start()
        return carry

    lax.fori_loop(0, heads, start_kv, 0)
    if ring:
        for copy in forward_copies(1):
            copy.start()
    lax.fori_loop(0, heads, functools.partial(start_q, chosen=(0, 1)), 0)
    lax.fori_loop(0, heads, functools.partial(start_q, chosen=(2,)), 0)
    for copy in parameters:
        copy.start()
    for j in range(1 if ring else n_blk):
        weight_local(j).start()
    for p in range(len(pieces)):
        residual_copy(p).start()

    for copy in parameters:
        copy.wait()
    head = wt_ref[...].astype(F32)
    for i, vector in enumerate((scale_ref, shift_ref)):
        head_rows[8 * i : 8 * i + 8] = lax.dot_general(
            jnp.broadcast_to(vector[...], (8, model)), head, (((1,), (1,)), ((), ())),
            precision=lax.Precision.HIGHEST, preferred_element_type=F32,
        )

    factor = math.log2(math.e) / math.sqrt(HD)

    def attend(h, c, at_chip):
        at = spots(at_chip, 2 * sizes[c])
        scores = lax.dot_general(
            queries[c][h, at, :], kv[0, h], (((1,), (1,)), ((), ())), preferred_element_type=F32
        )
        highest = jnp.max(scores, axis=-1, keepdims=True)
        exponent = jnp.exp2((scores - highest) * factor)
        denominator = jnp.sum(exponent, axis=-1, keepdims=True)
        summed = jnp.dot(exponent.astype(BF16), kv[1, h], preferred_element_type=F32)
        attended[c][at, pl.ds(pl.multiple_of(h * HD, HD), HD)] = (summed / denominator).astype(
            BF16
        )

    def near_head(h, carry):
        for t in range(2):
            for source in peers:
                kv_copy(t, h, source, 0, source).wait_recv()
            kv_own(t, h).wait()
        for p in range(len(pieces)):
            q_copy(p, h, sibling, 0, sibling).wait_recv()
            q_own(p, h).wait()
        for c in range(2):
            attend(h, c, chip)
        return carry

    def far_head(h, carry, c):
        for p, piece in enumerate(pieces):
            if piece[0] == c:
                for source in (far, far_sibling):
                    q_copy(p, h, source, 0, source).wait_recv()
        attend(h, c, far_chip)
        return carry

    early_heads = (heads * 3 + 4) // 5
    lax.fori_loop(0, early_heads, near_head, 0)
    if ring:
        for copy in forward_copies(1):
            copy.wait_recv()
        for copy in forward_copies(2):
            copy.start()
    lax.fori_loop(early_heads, heads, near_head, 0)
    lax.fori_loop(0, heads, functools.partial(far_head, c=0), 0)

    def part_copy(src, dst, send, recv, c, j, to):
        return pltpu.make_async_remote_copy(
            src_ref=src[c].at[j], dst_ref=dst[c].at[j], send_sem=send.at[c, j],
            recv_sem=recv.at[c, j], device_id={"fsdp": to}, device_id_type=MESH,
        )

    def side_copy(c, j):
        return part_copy(side_out, side_in, side_send, side_recv, c, j, sibling)

    def own_copy(c, j):
        return part_copy(own_out, own_in, own_send, own_recv, c, j, sibling)

    def cross_copy(c, j):
        return part_copy(cross_out, cross_in, cross_send, cross_recv, c, j, far)

    def project(c, j):
        size = sizes[c]
        mine_at, other_at = spots(core, size), spots(1 - core, size)
        far_hold[: 2 * size] = jnp.dot(
            attended[c][spots(far_chip, 2 * size), :], weights[j], preferred_element_type=F32
        )
        side_out[c][j] = far_hold[other_at, :].astype(BF16)
        side_copy(c, j).start()
        near_hold[: 2 * size] = jnp.dot(
            attended[c][spots(chip, 2 * size), :], weights[j], preferred_element_type=F32
        )
        own_out[c][j] = near_hold[other_at, :].astype(BF16)
        own_copy(c, j).start()
        side_copy(c, j).wait_recv()
        cross_out[c][j] = (far_hold[mine_at, :] + side_in[c][j].astype(F32)).astype(BF16)
        cross_copy(c, j).start()
        own_copy(c, j).wait_recv()
        hidden[c][j] = residual[c][:, columns(j)].astype(F32) + gate_ref[:, columns(j)] * (
            near_hold[mine_at, :] + own_in[c][j].astype(F32)
        )

    if ring:
        early = 2 * (half_ring - 2) + 1
        split = min(3, early)
        order = [(0, j) for j in range(early)] + [None] + [(1, j) for j in range(split)]
        order += [(0, j) for j in range(early, n_blk)] + [(1, j) for j in range(split, n_blk)]
    else:
        order = [(0, j) for j in range(n_blk)] + [None] + [(1, j) for j in range(n_blk)]

    for p in range(len(pieces)):
        residual_copy(p).wait()
    held = 1
    for step in order:
        if step is None:
            lax.fori_loop(0, heads, functools.partial(far_head, c=1), 0)
            continue
        c, j = step
        if c == 0 and (not ring or j == 0):
            weight_local(j).wait()
        if ring and (j + 1) // 2 > held:
            held = (j + 1) // 2
            for copy in forward_copies(held):
                copy.wait_recv()
            if held < half_ring:
                for copy in forward_copies(held + 1):
                    copy.start()
        project(c, j)

    state = [dict(raw=None, pivot=None, centres=[], spreads=[]) for _ in range(2)]

    def gather(c, j):
        now = state[c]
        cross_copy(c, j).wait_recv()
        block = hidden[c][j] + gate_ref[:, columns(j)] * cross_in[c][j].astype(F32)
        if now["pivot"] is None:
            now["pivot"] = jnp.sum(block, axis=-1, keepdims=True) * (1.0 / width)
        shifted = block - now["pivot"]
        term = lax.dot_general(
            (shifted * scale_ref[:, columns(j)]).astype(BF16), wt_ref[:, columns(j)],
            (((1,), (1,)), ((), ())), preferred_element_type=F32,
        )
        now["raw"] = term if now["raw"] is None else now["raw"] + term
        centre = jnp.sum(shifted, axis=-1, keepdims=True) * (1.0 / width)
        centred = shifted - centre
        now["centres"].append(centre)
        now["spreads"].append(jnp.sum(centred * centred, axis=-1, keepdims=True))

    step_size = step_ref[0]
    chunk_frames = (2 * FD, frames - 2 * FD)
    index = lax.broadcasted_iota(jnp.int32, (2 * FD, 1), 0)
    first_half = index < FD

    def pick(c, at):
        if c == 0:
            return jnp.where(first_half, lat_ref[: 2 * FD, at], lat_ref[frames - 2 * FD :, at])
        spread_over = pltpu.roll(
            jnp.where(first_half, lat_ref[frames - 2 * FD :, at], lat_ref[: 2 * FD, at]), FD, 0
        )
        return spread_over

    def freshen(c):
        now = state[c]
        mean = functools.reduce(jnp.add, now["centres"]) * (1.0 / n_blk)
        spread = functools.reduce(jnp.add, now["spreads"])
        for centre in now["centres"]:
            spread = spread + width * (centre - mean) * (centre - mean)
        inverse = 1.0 / jnp.sqrt(spread * (1.0 / (width * n_blk)) + EPSILON)
        flat[c][:, :channels] = inverse * (now["raw"] - mean * head_rows[:1]) + head_rows[8:9]
        for p in range(0, per_frame, 2):
            pair_of = jnp.concatenate(
                [
                    flat[c][pl.ds(p + i, chunk_frames[c], stride=per_frame), :][:, :channels]
                    for i in range(2)
                ],
                axis=1,
            )
            at = pl.ds(p * channels, 2 * channels)
            mine[c][:, at] = pick(c, at) + step_size * pair_of

    def edge_copy(dst, slot, to):
        return pltpu.make_async_remote_copy(
            src_ref=mine[0], dst_ref=dst, send_sem=edge_send.at[slot], recv_sem=edge_recv.at[slot],
            device_id={"win": to}, device_id_type=MESH,
        )

    edges = (edge_copy(before, 0, up_win), edge_copy(after, 1, down_win))

    def blend():
        edge = 2 * FD
        over_prev, over_next = inter_ref[down_win], inter_ref[win]
        zero = jnp.zeros((edge, 1), jnp.int32)
        theirs_w, own_w = zero, zero
        for i in range(FD):
            hit = (index == i) & (index < over_prev)
            theirs_w = jnp.where(hit, ramps_ref[2 * i, down_win], theirs_w)
            own_w = jnp.where(hit, ramps_ref[2 * i + 1, down_win], own_w)
            hit = index == edge - over_next + i
            own_w = jnp.where(hit, ramps_ref[2 * i, win], own_w)
            theirs_w = jnp.where(hit, ramps_ref[2 * i + 1, win], theirs_w)
        aligned = jnp.zeros((edge, wide), F32)
        earlier, later = before[...], after[...]
        for o in range(1, FD + 1):
            hit = first_half & ((zero + over_prev) == o)
            aligned = jnp.where(hit, pltpu.roll(earlier, o, 0), aligned)
            hit = jnp.logical_not(first_half) & ((zero + over_next) == o)
            aligned = jnp.where(hit, pltpu.roll(later, edge - o, 0), aligned)
        theirs = theirs_w.astype(F32)
        own = jnp.where(own_w > 0, own_w, 1).astype(F32)
        mine[0][...] = (theirs * aligned + own * mine[0][...]) / (theirs + own)

    steps = [step for step in order if step is not None]
    a_done = max(i for i, step in enumerate(steps) if step[0] == 0)
    for c, j in [step for step in steps[: a_done + 1] if step[0] == 0]:
        gather(c, j)
    freshen(0)
    for copy in edges:
        copy.start()
    b_steps = [step for step in steps if step[0] == 1]
    for c, j in b_steps[:-2]:
        gather(c, j)
    for copy in edges:
        copy.wait()
    blend()
    for c, j in b_steps[-2:]:
        gather(c, j)
    freshen(1)

    turned = pltpu.roll(mine[1][...], FD, 0)
    out_ref[: 2 * FD, :] = jnp.where(first_half, mine[0][...], turned)
    out_ref[frames - 2 * FD :, :] = jnp.where(first_half, turned, mine[0][...])

    def finish_head(h, carry):
        for slot, peer in enumerate(peers):
            for t in range(2):
                kv_copy(t, h, peer, slot).wait_send()
            for p in range(len(pieces)):
                q_copy(p, h, peer, slot).wait_send()
        return carry

    lax.fori_loop(0, heads, finish_head, 0)
    if ring:
        for s in range(1, half_ring + 1):
            for copy in forward_copies(s):
                copy.wait_send()
    for c in range(2):
        for j in range(n_blk):
            side_copy(c, j).wait_send()
            own_copy(c, j).wait_send()
            cross_copy(c, j).wait_send()


def local(
    queries,
    keys,
    values,
    stream,
    out_weight,
    gate,
    head_shift,
    head_scale,
    head_weight,
    latents,
    step_size,
    intersections,
    ramps,
):
    rows, features = queries.shape
    groups, n_win = lax.axis_size("fsdp"), lax.axis_size("win")
    heads = features // HD // groups
    depth, part = out_weight.shape
    model = stream.shape[1]
    ring = part % 128 == 0 and n_win % 2 == 0 and n_win >= 6
    if ring:
        n_blk, width = n_win, part
    else:
        n_blk = 8
        width = model // n_blk
        out_weight = lax.all_gather(out_weight, "win", axis=1, tiled=True)
    frames, wide = latents.shape
    assert frames == 4 * FD
    channels = head_weight.shape[1]
    ends = FD * (rows // frames)
    sizes = (2 * ends, rows - 2 * ends)
    any_spec = pl.BlockSpec(memory_space=pl.ANY)
    vmem = pl.BlockSpec(memory_space=pltpu.VMEM)
    smem = pl.BlockSpec(memory_space=pltpu.SMEM)
    dma = pltpu.SemaphoreType.DMA

    def both(shape, dtype):
        return tuple(pltpu.VMEM(shape(size), dtype) for size in sizes)

    parts = both(lambda size: (n_blk, size, width), BF16)
    hold = pltpu.VMEM((2 * max(sizes), width), F32)
    edge = pltpu.VMEM((2 * FD, wide), F32)
    return pl.pallas_call(
        functools.partial(kernel, ring, n_blk),
        out_shape=jax.ShapeDtypeStruct(latents.shape, latents.dtype),
        in_specs=[any_spec] * 10 + [smem] * 3,
        out_specs=vmem,
        scratch_shapes=[
            pltpu.VMEM((2, heads, groups * rows, HD), BF16),
            both(lambda size: (heads, groups * size, HD), BF16),
            both(lambda size: (groups * size, heads * HD), BF16),
            pltpu.VMEM((n_blk, depth, width), BF16),
            both(lambda size: (size, model), BF16),
            hold, hold,
            parts, parts, parts, parts, parts, parts,
            both(lambda size: (n_blk, size, width), F32),
            both(lambda size: (size, 128), F32),
            (edge, pltpu.VMEM((frames - 2 * FD, wide), F32)),
            edge, edge,
            pltpu.VMEM((16, channels), F32),
            pltpu.VMEM((1, model), F32),
            pltpu.VMEM((1, model), F32),
            pltpu.VMEM((1, model), F32),
            pltpu.VMEM((channels, model), head_weight.dtype),
            pltpu.VMEM((frames, wide), F32),
            dma((2, heads, 3)), dma((2, heads, groups)), dma((2, heads)),
            dma((3, heads, 3)), dma((3, heads, groups)), dma((3, heads)),
            dma((n_blk,)), dma((n_blk,)), dma((n_blk,)), dma((3,)), dma((5,)),
            dma((2, n_blk)), dma((2, n_blk)), dma((2, n_blk)), dma((2, n_blk)),
            dma((2, n_blk)), dma((2, n_blk)), dma((2,)), dma((2,)),
        ],
        compiler_params=pltpu.CompilerParams(
            collective_id=0, has_side_effects=True, vmem_limit_bytes=60 * 1024 * 1024
        ),
    )(
        queries, keys, values, stream, out_weight,
        gate[None, :], head_shift[None, :], head_scale[None, :], head_weight.T, latents,
        step_size, intersections, jnp.transpose(ramps, (1, 2, 0)).reshape(-1, n_win),
    )


def solution(mesh):
    in_specs = (
        P(("win", "fsdp"), None),
        P(("win", "fsdp"), None),
        P(("win", "fsdp"), None),
        P(("win", "fsdp"), None),
        P("fsdp", "win"),
        P(),
        P(),
        P(),
        P(),
        P("win", "fsdp"),
        P(),
        P(),
        P(),
    )
    out_specs = P("win", "fsdp")
    return jax.shard_map(local, mesh=mesh, in_specs=in_specs, out_specs=out_specs, check_vma=False)
```

time: 122 us -> 114 us (0.934)
  Pallas kernels: 120 us -> 112 us
    pallas_call x1, Pallas kernels: 120 us -> 112 us  [local(): pl.pallas_call(functools.partial(kernel, ring, n_blk), out_shape=jax.Shap...]
where the time goes in v1:
time: 114 us
  Pallas kernels  112 us (98%)
  local copies, waits for them, and re-layouts  1.47 us (1%)
    pallas_call x1, Pallas kernels, local(): pl.pallas_call(functools.partial(kernel, ring, n_blk), out_shape=jax.Shap...  112 us

profile of v1, /device:TPU:0, one launch (start us, length us, event | category | flops | bytes accessed | tf_op | source)
XLA Modules:
  0.0 113.7 jit_solution(15240122222352655909)
XLA Ops:
  0.7 111.5 %shard_map.127 = f32[16,1024]{1,0:T(8,128)} custom-call(bf16[256,2560]{1,0:T(8,128)(2,1)} %q_ref.1, bf16[256,2560]{1,0:T(8,128)(2,1)} %k_ref.1, bf16[256,2560]{1,0:T(8,128)(2,1)} %v_ref.1, bf16[256,5120]{1,0:T(8,128)(2,1)} %stream_ref.1, bf16[640,640]{1,0:T(8,128)(2,1)} %ow_ref.1, f32[1,5120]{1,0:T(1,128)} %bitcast.8, f32[1,5120]{1,0:T(1,128)} %bitcast.9, ...), custom_call_target="tpu_custom_call" | custom-call | tf_op jit(solution)/shard_map/pallas_call | solution.py:490
  112.2 1.5 %copy.16 = f32[16,1024]{1,0:T(8,128)} copy(f32[16,1024]{1,0:T(8,128)} %shard_map.127) | data formatting | bytes 131072

commit v2 on v1

--- a/solution.py
+++ b/solution.py
@@ -19,12 +19,12 @@
 
 def kernel(
     ring, n_blk, q_ref, k_ref, v_ref, stream_ref, ow_ref, gate_hbm, shift_hbm, scale_hbm, wt_hbm,
-    lat_hbm, step_ref, inter_ref, ramps_ref, out_ref,
+    lat_hbm, step_hbm, inter_hbm, ramps_hbm, out_hbm,
     kv, queries, attended, weights, residual, far_hold, near_hold, side_out, side_in, own_out,
     own_in, cross_out, cross_in, hidden, flat, mine, before, after, head_rows,
-    gate_ref, shift_ref, scale_ref, wt_ref, lat_ref,
-    kv_send, kv_recv, kv_local, q_send, q_recv, q_local, w_send, w_recv, w_local, res_sem,
-    par_sem, side_send, side_recv, own_send, own_recv, cross_send, cross_recv, edge_send,
+    gate_ref, shift_ref, scale_ref, wt_ref, lat_ref, step_ref, inter_ref, ramps_ref, out_ref,
+    kv_send, kv_recv, q_near, q_far, own_sem, w_send, w_recv, w_local, res_sem,
+    par_sem, out_sem, side_send, side_recv, own_send, own_recv, cross_send, cross_recv, edge_send,
     edge_recv,
 ):
     win, n_win = lax.axis_index("win"), lax.axis_size("win")
@@ -85,30 +85,29 @@
     peers = (far, far_sibling, sibling)
     pair = (k_ref, v_ref)
 
-    def kv_copy(t, h, to, slot, source=None):
-        source = me if source is None else source
+    def kv_copy(t, h, to, slot):
         return pltpu.make_async_remote_copy(
             src_ref=pair[t].at[:, head_columns(to, h)],
-            dst_ref=kv.at[t, h, spots(source, rows), :],
-            send_sem=kv_send.at[t, h, slot],
-            recv_sem=kv_recv.at[t, h, source],
+            dst_ref=kv.at[t, h, spots(me, rows), :],
+            send_sem=kv_send.at[t, slot],
+            recv_sem=kv_recv.at[h],
             device_id={"fsdp": to},
             device_id_type=MESH,
         )
 
     def kv_own(t, h):
         return pltpu.make_async_copy(
-            pair[t].at[:, head_columns(me, h)], kv.at[t, h, spots(me, rows), :], kv_local.at[t, h]
-        )
-
-    def q_copy(p, h, to, slot, source=None):
+            pair[t].at[:, head_columns(me, h)], kv.at[t, h, spots(me, rows), :], own_sem.at[0]
+        )
+
+    def q_copy(p, h, to, slot):
+        near = slot == 2
         chunk, first, start, length = pieces[p]
-        source = me if source is None else source
         return pltpu.make_async_remote_copy(
             src_ref=q_ref.at[pl.ds(first, length), head_columns(to, h)],
-            dst_ref=queries[chunk].at[h, spots(source, sizes[chunk], start, length), :],
-            send_sem=q_send.at[p, h, slot],
-            recv_sem=q_recv.at[p, h, source],
+            dst_ref=queries[chunk].at[h, spots(me, sizes[chunk], start, length), :],
+            send_sem=kv_send.at[2, slot],
+            recv_sem=q_near.at[0] if near else q_far.at[chunk, h],
             device_id={"fsdp": to},
             device_id_type=MESH,
         )
@@ -118,12 +117,12 @@
         return pltpu.make_async_copy(
             q_ref.at[pl.ds(first, length), head_columns(me, h)],
             queries[chunk].at[h, spots(me, sizes[chunk], start, length), :],
-            q_local.at[p, h],
+            own_sem.at[1],
         )
 
     def weight_copy(src, dst, slot, to):
         return pltpu.make_async_remote_copy(
-            src_ref=src, dst_ref=dst, send_sem=w_send.at[slot], recv_sem=w_recv.at[slot],
+            src_ref=src, dst_ref=dst, send_sem=w_send.at[0], recv_sem=w_recv.at[slot],
             device_id={"win": to}, device_id_type=MESH,
         )
 
@@ -146,7 +145,7 @@
 
     def weight_local(j):
         source = ow_ref if ring else ow_ref.at[:, columns(j)]
-        return pltpu.make_async_copy(source, weights.at[j], w_local.at[j])
+        return pltpu.make_async_copy(source, weights.at[j], w_local.at[0])
 
     def residual_copy(p):
         chunk, first, start, length = pieces[p]
@@ -165,6 +164,9 @@
                 (wt_hbm, wt_ref),
                 (gate_hbm, gate_ref),
                 (lat_hbm, lat_ref),
+                (step_hbm, step_ref),
+                (inter_hbm, inter_ref),
+                (ramps_hbm, ramps_ref),
             )
         )
     )
@@ -172,7 +174,7 @@
     barrier = pltpu.get_barrier_semaphore()
     for peer in peers:
         pl.semaphore_signal(barrier, inc=1, device_id={"fsdp": peer}, device_id_type=MESH)
-    greeted = [up_win, down_win] + ([ring_next, ring_prev] if ring else [])
+    greeted = [ring_next, ring_prev] if ring else [up_win, down_win]
     for other in greeted:
         pl.semaphore_signal(barrier, inc=1, device_id={"win": other}, device_id_type=MESH)
     pl.semaphore_wait(barrier, len(peers) + len(greeted))
@@ -215,6 +217,9 @@
 
     factor = math.log2(math.e) / math.sqrt(HD)
 
+    def await_bytes(like, sem):
+        pltpu.make_async_copy(like, like, sem).wait()
+
     def attend(h, c, at_chip):
         at = spots(at_chip, 2 * sizes[c])
         scores = lax.dot_general(
@@ -229,25 +234,20 @@
         )
 
     def near_head(h, carry):
-        for t in range(2):
-            for source in peers:
-                kv_copy(t, h, source, 0, source).wait_recv()
-            kv_own(t, h).wait()
-        for p in range(len(pieces)):
-            q_copy(p, h, sibling, 0, sibling).wait_recv()
-            q_own(p, h).wait()
+        await_bytes(kv.at[:, h, pl.ds(0, len(peers) * rows), :], kv_recv.at[h])
         for c in range(2):
             attend(h, c, chip)
         return carry
 
     def far_head(h, carry, c):
-        for p, piece in enumerate(pieces):
-            if piece[0] == c:
-                for source in (far, far_sibling):
-                    q_copy(p, h, source, 0, source).wait_recv()
+        await_bytes(queries[c].at[h, spots(far_chip, 2 * sizes[c]), :], q_far.at[c, h])
         attend(h, c, far_chip)
         return carry
 
+    own_part = pl.ds(0, rows)
+    await_bytes(kv.at[:, :, own_part, :], own_sem.at[0])
+    await_bytes(kv.at[0, :, own_part, :], own_sem.at[1])
+    await_bytes(kv.at[0, :, own_part, :], q_near.at[0])
     early_heads = (heads * 3 + 4) // 5
     lax.fori_loop(0, early_heads, near_head, 0)
     if ring:
@@ -258,20 +258,35 @@
     lax.fori_loop(early_heads, heads, near_head, 0)
     lax.fori_loop(0, heads, functools.partial(far_head, c=0), 0)
 
+    if ring:
+        early = 2 * (half_ring - 2) + 1
+        split = min(3, early)
+        order = [(0, j) for j in range(early)] + [None] + [(1, j) for j in range(split)]
+        order += [(0, j) for j in range(early, n_blk)] + [(1, j) for j in range(split, n_blk)]
+    else:
+        order = [(0, j) for j in range(n_blk)] + [None] + [(1, j) for j in range(n_blk)]
+
+    steps = [step for step in order if step is not None]
+    turn = {step: i for i, step in enumerate(steps)}
+    a_steps = [step for step in steps if step[0] == 0]
+    b_steps = [step for step in steps if step[0] == 1]
+    bins = [a_steps, b_steps[:-3]] + [[step] for step in b_steps[-3:]]
+    bin_of = {step: i for i, several in enumerate(bins) for step in several}
+
     def part_copy(src, dst, send, recv, c, j, to):
         return pltpu.make_async_remote_copy(
-            src_ref=src[c].at[j], dst_ref=dst[c].at[j], send_sem=send.at[c, j],
-            recv_sem=recv.at[c, j], device_id={"fsdp": to}, device_id_type=MESH,
+            src_ref=src[c].at[j], dst_ref=dst[c].at[j], send_sem=send.at[c], recv_sem=recv,
+            device_id={"fsdp": to}, device_id_type=MESH,
         )
 
     def side_copy(c, j):
-        return part_copy(side_out, side_in, side_send, side_recv, c, j, sibling)
+        return part_copy(side_out, side_in, side_send, side_recv.at[turn[c, j] % 2], c, j, sibling)
 
     def own_copy(c, j):
-        return part_copy(own_out, own_in, own_send, own_recv, c, j, sibling)
+        return part_copy(own_out, own_in, own_send, own_recv.at[turn[c, j] % 2], c, j, sibling)
 
     def cross_copy(c, j):
-        return part_copy(cross_out, cross_in, cross_send, cross_recv, c, j, far)
+        return part_copy(cross_out, cross_in, cross_send, cross_recv.at[bin_of[c, j]], c, j, far)
 
     def project(c, j):
         size = sizes[c]
@@ -294,24 +309,15 @@
             near_hold[mine_at, :] + own_in[c][j].astype(F32)
         )
 
-    if ring:
-        early = 2 * (half_ring - 2) + 1
-        split = min(3, early)
-        order = [(0, j) for j in range(early)] + [None] + [(1, j) for j in range(split)]
-        order += [(0, j) for j in range(early, n_blk)] + [(1, j) for j in range(split, n_blk)]
-    else:
-        order = [(0, j) for j in range(n_blk)] + [None] + [(1, j) for j in range(n_blk)]
-
     for p in range(len(pieces)):
         residual_copy(p).wait()
+    await_bytes(weights.at[: 1 if ring else n_blk], w_local.at[0])
     held = 1
     for step in order:
         if step is None:
             lax.fori_loop(0, heads, functools.partial(far_head, c=1), 0)
             continue
         c, j = step
-        if c == 0 and (not ring or j == 0):
-            weight_local(j).wait()
         if ring and (j + 1) // 2 > held:
             held = (j + 1) // 2
             for copy in forward_copies(held):
@@ -325,7 +331,6 @@
 
     def gather(c, j):
         now = state[c]
-        cross_copy(c, j).wait_recv()
         block = hidden[c][j] + gate_ref[:, columns(j)] * cross_in[c][j].astype(F32)
         if now["pivot"] is None:
             now["pivot"] = jnp.sum(block, axis=-1, keepdims=True) * (1.0 / width)
@@ -403,45 +408,40 @@
         own = jnp.where(own_w > 0, own_w, 1).astype(F32)
         mine[0][...] = (theirs * aligned + own * mine[0][...]) / (theirs + own)
 
-    steps = [step for step in order if step is not None]
-    a_done = max(i for i, step in enumerate(steps) if step[0] == 0)
-    for c, j in [step for step in steps[: a_done + 1] if step[0] == 0]:
-        gather(c, j)
+    def gather_bin(i):
+        c = bins[i][0][0]
+        await_bytes(cross_in[c].at[: len(bins[i])], cross_recv.at[i])
+        for step in bins[i]:
+            gather(*step)
+
+    gather_bin(0)
     freshen(0)
     for copy in edges:
         copy.start()
-    b_steps = [step for step in steps if step[0] == 1]
-    for c, j in b_steps[:-2]:
-        gather(c, j)
+    gather_bin(1)
+    gather_bin(2)
     for copy in edges:
         copy.wait()
     blend()
-    for c, j in b_steps[-2:]:
-        gather(c, j)
+    gather_bin(3)
+    gather_bin(4)
     freshen(1)
 
     turned = pltpu.roll(mine[1][...], FD, 0)
     out_ref[: 2 * FD, :] = jnp.where(first_half, mine[0][...], turned)
     out_ref[frames - 2 * FD :, :] = jnp.where(first_half, turned, mine[0][...])
-
-    def finish_head(h, carry):
-        for slot, peer in enumerate(peers):
-            for t in range(2):
-                kv_copy(t, h, peer, slot).wait_send()
-            for p in range(len(pieces)):
-                q_copy(p, h, peer, slot).wait_send()
-        return carry
-
-    lax.fori_loop(0, heads, finish_head, 0)
+    result = pltpu.make_async_copy(out_ref, out_hbm, out_sem.at[0])
+    result.start()
+
+    for t in range(3):
+        for slot in range(len(peers)):
+            await_bytes(kv.at[0, :, own_part, :], kv_send.at[t, slot])
     if ring:
-        for s in range(1, half_ring + 1):
-            for copy in forward_copies(s):
-                copy.wait_send()
+        await_bytes(weights.at[:last], w_send.at[0])
     for c in range(2):
-        for j in range(n_blk):
-            side_copy(c, j).wait_send()
-            own_copy(c, j).wait_send()
-            cross_copy(c, j).wait_send()
+        for send in (side_send, own_send, cross_send):
+            await_bytes(cross_in[c], send.at[c])
+    result.wait()
 
 
 def local(
@@ -477,8 +477,6 @@
     ends = FD * (rows // frames)
     sizes = (2 * ends, rows - 2 * ends)
     any_spec = pl.BlockSpec(memory_space=pl.ANY)
-    vmem = pl.BlockSpec(memory_space=pltpu.VMEM)
-    smem = pl.BlockSpec(memory_space=pltpu.SMEM)
     dma = pltpu.SemaphoreType.DMA
 
     def both(shape, dtype):
@@ -490,8 +488,8 @@
     return pl.pallas_call(
         functools.partial(kernel, ring, n_blk),
         out_shape=jax.ShapeDtypeStruct(latents.shape, latents.dtype),
-        in_specs=[any_spec] * 10 + [smem] * 3,
-        out_specs=vmem,
+        in_specs=[any_spec] * 13,
+        out_specs=any_spec,
         scratch_shapes=[
             pltpu.VMEM((2, heads, groups * rows, HD), BF16),
             both(lambda size: (heads, groups * size, HD), BF16),
@@ -510,11 +508,14 @@
             pltpu.VMEM((1, model), F32),
             pltpu.VMEM((channels, model), head_weight.dtype),
             pltpu.VMEM((frames, wide), F32),
-            dma((2, heads, 3)), dma((2, heads, groups)), dma((2, heads)),
-            dma((3, heads, 3)), dma((3, heads, groups)), dma((3, heads)),
-            dma((n_blk,)), dma((n_blk,)), dma((n_blk,)), dma((3,)), dma((5,)),
-            dma((2, n_blk)), dma((2, n_blk)), dma((2, n_blk)), dma((2, n_blk)),
-            dma((2, n_blk)), dma((2, n_blk)), dma((2,)), dma((2,)),
+            pltpu.SMEM((1,), F32),
+            pltpu.SMEM((n_win,), jnp.int32),
+            pltpu.SMEM((2 * FD, n_win), jnp.int32),
+            pltpu.VMEM((frames, wide), F32),
+            dma((3, 3)), dma((heads,)), dma((1,)), dma((2, heads)), dma((2,)),
+            dma((1,)), dma((n_blk,)), dma((1,)), dma((3,)), dma((8,)), dma((1,)),
+            dma((2,)), dma((2,)), dma((2,)), dma((2,)),
+            dma((2,)), dma((5,)), dma((2,)), dma((2,)),
         ],
         compiler_params=pltpu.CompilerParams(
             collective_id=0, has_side_effects=True, vmem_limit_bytes=60 * 1024 * 1024

time: 114 us -> 107 us (0.939)
  Pallas kernels: 112 us -> 105 us
    pallas_call x1, Pallas kernels: 112 us -> 105 us  [local(): pl.pallas_call(functools.partial(kernel, ring, n_blk), out_shape=jax.Shap...]
where the time goes in v2:
time: 107 us
  Pallas kernels  105 us (98%)
  local copies, waits for them, and re-layouts  1.47 us (1%)
    pallas_call x1, Pallas kernels, local(): pl.pallas_call(functools.partial(kernel, ring, n_blk), out_shape=jax.Shap...  105 us

profile of v2, /device:TPU:0, one launch (start us, length us, event | category | flops | bytes accessed | tf_op | source)
XLA Modules:
  0.0 107.3 jit_solution(4536693546355004902)
XLA Ops:
  0.7 105.2 %shard_map.127 = f32[16,1024]{1,0:T(8,128)} custom-call(bf16[256,2560]{1,0:T(8,128)(2,1)} %q_ref.1, bf16[256,2560]{1,0:T(8,128)(2,1)} %k_ref.1, bf16[256,2560]{1,0:T(8,128)(2,1)} %v_ref.1, bf16[256,5120]{1,0:T(8,128)(2,1)} %stream_ref.1, bf16[640,640]{1,0:T(8,128)(2,1)} %ow_ref.1, f32[1,5120]{1,0:T(1,128)} %bitcast.8, f32[1,5120]{1,0:T(1,128)} %bitcast.9, ...), custom_call_target="tpu_custom_call" | custom-call | tf_op jit(solution)/shard_map/pallas_call | solution.py:488
  105.8 1.5 %copy.16 = f32[16,1024]{1,0:T(8,128)} copy(f32[16,1024]{1,0:T(8,128)} %shard_map.127) | data formatting | bytes 131072

commit v3 on v2

--- a/solution.py
+++ b/solution.py
@@ -19,12 +19,12 @@
 
 def kernel(
     ring, n_blk, q_ref, k_ref, v_ref, stream_ref, ow_ref, gate_hbm, shift_hbm, scale_hbm, wt_hbm,
-    lat_hbm, step_hbm, inter_hbm, ramps_hbm, out_hbm,
+    lat_hbm, step_hbm, inter_hbm, ramps_hbm, out_ref,
     kv, queries, attended, weights, residual, far_hold, near_hold, side_out, side_in, own_out,
     own_in, cross_out, cross_in, hidden, flat, mine, before, after, head_rows,
-    gate_ref, shift_ref, scale_ref, wt_ref, lat_ref, step_ref, inter_ref, ramps_ref, out_ref,
+    gate_ref, shift_ref, scale_ref, wt_ref, lat_ref, step_ref, inter_ref, ramps_ref,
     kv_send, kv_recv, q_near, q_far, own_sem, w_send, w_recv, w_local, res_sem,
-    par_sem, out_sem, side_send, side_recv, own_send, own_recv, cross_send, cross_recv, edge_send,
+    par_sem, side_send, side_recv, own_send, own_recv, cross_send, cross_recv, edge_send,
     edge_recv,
 ):
     win, n_win = lax.axis_index("win"), lax.axis_size("win")
@@ -430,8 +430,6 @@
     turned = pltpu.roll(mine[1][...], FD, 0)
     out_ref[: 2 * FD, :] = jnp.where(first_half, mine[0][...], turned)
     out_ref[frames - 2 * FD :, :] = jnp.where(first_half, turned, mine[0][...])
-    result = pltpu.make_async_copy(out_ref, out_hbm, out_sem.at[0])
-    result.start()
 
     for t in range(3):
         for slot in range(len(peers)):
@@ -441,7 +439,6 @@
     for c in range(2):
         for send in (side_send, own_send, cross_send):
             await_bytes(cross_in[c], send.at[c])
-    result.wait()
 
 
 def local(
@@ -487,9 +484,9 @@
     edge = pltpu.VMEM((2 * FD, wide), F32)
     return pl.pallas_call(
         functools.partial(kernel, ring, n_blk),
-        out_shape=jax.ShapeDtypeStruct(latents.shape, latents.dtype),
+        out_shape=pltpu.VMEM(latents.shape, latents.dtype),
         in_specs=[any_spec] * 13,
-        out_specs=any_spec,
+        out_specs=pl.BlockSpec(memory_space=pltpu.VMEM),
         scratch_shapes=[
             pltpu.VMEM((2, heads, groups * rows, HD), BF16),
             both(lambda size: (heads, groups * size, HD), BF16),
@@ -511,9 +508,8 @@
             pltpu.SMEM((1,), F32),
             pltpu.SMEM((n_win,), jnp.int32),
             pltpu.SMEM((2 * FD, n_win), jnp.int32),
-            pltpu.VMEM((frames, wide), F32),
             dma((3, 3)), dma((heads,)), dma((1,)), dma((2, heads)), dma((2,)),
-            dma((1,)), dma((n_blk,)), dma((1,)), dma((3,)), dma((8,)), dma((1,)),
+            dma((1,)), dma((n_blk,)), dma((1,)), dma((3,)), dma((8,)),
             dma((2,)), dma((2,)), dma((2,)), dma((2,)),
             dma((2,)), dma((5,)), dma((2,)), dma((2,)),
         ],

time: 107 us -> 106 us (level)
  no operation moved by 1% of the time
where the time goes in v3:
time: 106 us
  Pallas kernels  105 us (99%)
    pallas_call x1, Pallas kernels, local(): pl.pallas_call(functools.partial(kernel, ring, n_blk), out_shape=pltpu.VM...  105 us

profile of v3, /device:TPU:0, one launch (start us, length us, event | category | flops | bytes accessed | tf_op | source)
XLA Modules:
  0.0 105.9 jit_solution(6442066283846054039)
XLA Ops:
  0.7 104.6 %shard_map.127 = f32[16,1024]{1,0:T(8,128)S(1)} custom-call(bf16[256,2560]{1,0:T(8,128)(2,1)} %q_ref.1, bf16[256,2560]{1,0:T(8,128)(2,1)} %k_ref.1, bf16[256,2560]{1,0:T(8,128)(2,1)} %v_ref.1, bf16[256,5120]{1,0:T(8,128)(2,1)} %stream_ref.1, bf16[640,640]{1,0:T(8,128)(2,1)} %ow_ref.1, f32[1,5120]{1,0:T(1,128)} %bitcast.8, f32[1,5120]{1,0:T(1,128)} %bitcast.9, ...), custom_call_target="tpu_custom_call" | custom-call | tf_op jit(solution)/shard_map/pallas_call | solution.py:485
  105.2 0.6 copy.15

commit v4 on v3

--- a/solution.py
+++ b/solution.py
@@ -21,10 +21,10 @@
     ring, n_blk, q_ref, k_ref, v_ref, stream_ref, ow_ref, gate_hbm, shift_hbm, scale_hbm, wt_hbm,
     lat_hbm, step_hbm, inter_hbm, ramps_hbm, out_ref,
     kv, queries, attended, weights, residual, far_hold, near_hold, side_out, side_in, own_out,
-    own_in, cross_out, cross_in, hidden, flat, mine, before, after, head_rows,
-    gate_ref, shift_ref, scale_ref, wt_ref, lat_ref, step_ref, inter_ref, ramps_ref,
-    kv_send, kv_recv, q_near, q_far, own_sem, w_send, w_recv, w_local, res_sem,
-    par_sem, side_send, side_recv, own_send, own_recv, cross_send, cross_recv, edge_send,
+    own_in, cross_out, cross_in, hidden, flat, mine, around, head_rows,
+    staged, vectors, wt_ref, lat_ref, step_ref, inter_ref, ramps_ref, stage_sem,
+    kv_send, kv_recv, q_far, own_sem, w_send, w_recv, w_local, res_sem,
+    par_sem, part_send, side_recv, own_recv, cross_recv, edge_send,
     edge_recv,
 ):
     win, n_win = lax.axis_index("win"), lax.axis_size("win")
@@ -83,13 +83,14 @@
         return pl.ds(pl.multiple_of(device * size + start, math.gcd(size, start)), length)
 
     peers = (far, far_sibling, sibling)
-    pair = (k_ref, v_ref)
+    pair = (staged.at[0], staged.at[1])
+    scale_ref, shift_ref, gate_ref = (vectors.at[i] for i in range(3))
 
     def kv_copy(t, h, to, slot):
         return pltpu.make_async_remote_copy(
             src_ref=pair[t].at[:, head_columns(to, h)],
             dst_ref=kv.at[t, h, spots(me, rows), :],
-            send_sem=kv_send.at[t, slot],
+            send_sem=kv_send.at[0],
             recv_sem=kv_recv.at[h],
             device_id={"fsdp": to},
             device_id_type=MESH,
@@ -104,10 +105,10 @@
         near = slot == 2
         chunk, first, start, length = pieces[p]
         return pltpu.make_async_remote_copy(
-            src_ref=q_ref.at[pl.ds(first, length), head_columns(to, h)],
+            src_ref=staged.at[2, pl.ds(first, length), head_columns(to, h)],
             dst_ref=queries[chunk].at[h, spots(me, sizes[chunk], start, length), :],
-            send_sem=kv_send.at[2, slot],
-            recv_sem=q_near.at[0] if near else q_far.at[chunk, h],
+            send_sem=kv_send.at[1],
+            recv_sem=own_sem.at[1] if near else q_far.at[h if chunk == 0 else heads],
             device_id={"fsdp": to},
             device_id_type=MESH,
         )
@@ -115,14 +116,14 @@
     def q_own(p, h):
         chunk, first, start, length = pieces[p]
         return pltpu.make_async_copy(
-            q_ref.at[pl.ds(first, length), head_columns(me, h)],
+            staged.at[2, pl.ds(first, length), head_columns(me, h)],
             queries[chunk].at[h, spots(me, sizes[chunk], start, length), :],
             own_sem.at[1],
         )
 
     def weight_copy(src, dst, slot, to):
         return pltpu.make_async_remote_copy(
-            src_ref=src, dst_ref=dst, send_sem=w_send.at[0], recv_sem=w_recv.at[slot],
+            src_ref=src, dst_ref=dst, send_sem=w_send.at[0], recv_sem=w_recv.at[slot // 2],
             device_id={"win": to}, device_id_type=MESH,
         )
 
@@ -143,6 +144,10 @@
             weight_copy(weights.at[2 * s - 2, low], weights.at[last, low], 2 * s - 1, ring_prev),
         )
 
+    def await_weights(s):
+        some = weights.at[2 * s - 1 : 2 * s + 1] if s < half_ring else weights.at[last:]
+        await_bytes(some, w_recv.at[s - 1])
+
     def weight_local(j):
         source = ow_ref if ring else ow_ref.at[:, columns(j)]
         return pltpu.make_async_copy(source, weights.at[j], w_local.at[0])
@@ -152,24 +157,35 @@
         return pltpu.make_async_copy(
             stream_ref.at[pl.ds(first, length), :],
             residual[chunk].at[pl.ds(start, length), :],
-            res_sem.at[p],
-        )
-
-    parameters = tuple(
-        pltpu.make_async_copy(src, dst, par_sem.at[i])
+            res_sem.at[0],
+        )
+
+    loads = [
+        pltpu.make_async_copy(src, vectors.at[i], par_sem.at[0])
+        for i, src in enumerate((scale_hbm, shift_hbm, gate_hbm))
+    ]
+    others = [
+        pltpu.make_async_copy(src, dst, par_sem.at[1 + i])
         for i, (src, dst) in enumerate(
             (
-                (scale_hbm, scale_ref),
-                (shift_hbm, shift_ref),
                 (wt_hbm, wt_ref),
-                (gate_hbm, gate_ref),
                 (lat_hbm, lat_ref),
                 (step_hbm, step_ref),
                 (inter_hbm, inter_ref),
                 (ramps_hbm, ramps_ref),
             )
         )
+    ]
+
+    stages = tuple(
+        pltpu.make_async_copy(src, staged.at[i], stage_sem.at[min(i, 1)])
+        for i, src in enumerate((k_ref, v_ref, q_ref))
     )
+    for copy in stages:
+        copy.start()
+
+    def await_bytes(like, sem):
+        pltpu.make_async_copy(like, like, sem).wait()
 
     barrier = pltpu.get_barrier_semaphore()
     for peer in peers:
@@ -179,11 +195,10 @@
         pl.semaphore_signal(barrier, inc=1, device_id={"win": other}, device_id_type=MESH)
     pl.semaphore_wait(barrier, len(peers) + len(greeted))
 
-    def start_kv(h, carry):
-        for t in range(2):
-            for slot, peer in enumerate(peers):
-                kv_copy(t, h, peer, slot).start()
-            kv_own(t, h).start()
+    def start_kv(h, carry, t):
+        for slot, peer in enumerate(peers):
+            kv_copy(t, h, peer, slot).start()
+        kv_own(t, h).start()
         return carry
 
     def start_q(h, carry, chosen):
@@ -193,20 +208,24 @@
             q_own(p, h).start()
         return carry
 
-    lax.fori_loop(0, heads, start_kv, 0)
+    stages[0].wait()
+    lax.fori_loop(0, heads, functools.partial(start_kv, t=0), 0)
+    await_bytes(staged.at[1:], stage_sem.at[1])
+    lax.fori_loop(0, heads, functools.partial(start_kv, t=1), 0)
     if ring:
         for copy in forward_copies(1):
             copy.start()
     lax.fori_loop(0, heads, functools.partial(start_q, chosen=(0, 1)), 0)
     lax.fori_loop(0, heads, functools.partial(start_q, chosen=(2,)), 0)
-    for copy in parameters:
+    for copy in loads + others:
         copy.start()
     for j in range(1 if ring else n_blk):
         weight_local(j).start()
     for p in range(len(pieces)):
         residual_copy(p).start()
 
-    for copy in parameters:
+    await_bytes(vectors, par_sem.at[0])
+    for copy in others:
         copy.wait()
     head = wt_ref[...].astype(F32)
     for i, vector in enumerate((scale_ref, shift_ref)):
@@ -216,10 +235,6 @@
         )
 
     factor = math.log2(math.e) / math.sqrt(HD)
-
-    def await_bytes(like, sem):
-        pltpu.make_async_copy(like, like, sem).wait()
-
     def attend(h, c, at_chip):
         at = spots(at_chip, 2 * sizes[c])
         scores = lax.dot_general(
@@ -240,22 +255,19 @@
         return carry
 
     def far_head(h, carry, c):
-        await_bytes(queries[c].at[h, spots(far_chip, 2 * sizes[c]), :], q_far.at[c, h])
+        if c == 0:
+            await_bytes(queries[c].at[h, spots(far_chip, 2 * sizes[c]), :], q_far.at[h])
         attend(h, c, far_chip)
         return carry
 
     own_part = pl.ds(0, rows)
     await_bytes(kv.at[:, :, own_part, :], own_sem.at[0])
-    await_bytes(kv.at[0, :, own_part, :], own_sem.at[1])
-    await_bytes(kv.at[0, :, own_part, :], q_near.at[0])
-    early_heads = (heads * 3 + 4) // 5
-    lax.fori_loop(0, early_heads, near_head, 0)
+    await_bytes(kv.at[:, :, own_part, :], own_sem.at[1])
     if ring:
-        for copy in forward_copies(1):
-            copy.wait_recv()
+        await_weights(1)
         for copy in forward_copies(2):
             copy.start()
-    lax.fori_loop(early_heads, heads, near_head, 0)
+    lax.fori_loop(0, heads, near_head, 0)
     lax.fori_loop(0, heads, functools.partial(far_head, c=0), 0)
 
     if ring:
@@ -275,18 +287,18 @@
 
     def part_copy(src, dst, send, recv, c, j, to):
         return pltpu.make_async_remote_copy(
-            src_ref=src[c].at[j], dst_ref=dst[c].at[j], send_sem=send.at[c], recv_sem=recv,
+            src_ref=src[c].at[j], dst_ref=dst[c].at[j], send_sem=part_send.at[c, send], recv_sem=recv,
             device_id={"fsdp": to}, device_id_type=MESH,
         )
 
     def side_copy(c, j):
-        return part_copy(side_out, side_in, side_send, side_recv.at[turn[c, j] % 2], c, j, sibling)
+        return part_copy(side_out, side_in, 0, side_recv.at[turn[c, j] % 2], c, j, sibling)
 
     def own_copy(c, j):
-        return part_copy(own_out, own_in, own_send, own_recv.at[turn[c, j] % 2], c, j, sibling)
+        return part_copy(own_out, own_in, 0, own_recv.at[turn[c, j] % 2], c, j, sibling)
 
     def cross_copy(c, j):
-        return part_copy(cross_out, cross_in, cross_send, cross_recv.at[bin_of[c, j]], c, j, far)
+        return part_copy(cross_out, cross_in, 1, cross_recv.at[bin_of[c, j]], c, j, far_sibling)
 
     def project(c, j):
         size = sizes[c]
@@ -294,7 +306,7 @@
         far_hold[: 2 * size] = jnp.dot(
             attended[c][spots(far_chip, 2 * size), :], weights[j], preferred_element_type=F32
         )
-        side_out[c][j] = far_hold[other_at, :].astype(BF16)
+        side_out[c][j] = far_hold[mine_at, :].astype(BF16)
         side_copy(c, j).start()
         near_hold[: 2 * size] = jnp.dot(
             attended[c][spots(chip, 2 * size), :], weights[j], preferred_element_type=F32
@@ -302,26 +314,26 @@
         own_out[c][j] = near_hold[other_at, :].astype(BF16)
         own_copy(c, j).start()
         side_copy(c, j).wait_recv()
-        cross_out[c][j] = (far_hold[mine_at, :] + side_in[c][j].astype(F32)).astype(BF16)
+        cross_out[c][j] = (far_hold[other_at, :] + side_in[c][j].astype(F32)).astype(BF16)
         cross_copy(c, j).start()
         own_copy(c, j).wait_recv()
         hidden[c][j] = residual[c][:, columns(j)].astype(F32) + gate_ref[:, columns(j)] * (
             near_hold[mine_at, :] + own_in[c][j].astype(F32)
         )
 
-    for p in range(len(pieces)):
-        residual_copy(p).wait()
+    await_bytes(stream_ref, res_sem.at[0])
     await_bytes(weights.at[: 1 if ring else n_blk], w_local.at[0])
     held = 1
     for step in order:
         if step is None:
+            far_rows = spots(far_chip, 2 * sizes[1])
+            await_bytes(queries[1].at[:, far_rows, :], q_far.at[heads])
             lax.fori_loop(0, heads, functools.partial(far_head, c=1), 0)
             continue
         c, j = step
         if ring and (j + 1) // 2 > held:
             held = (j + 1) // 2
-            for copy in forward_copies(held):
-                copy.wait_recv()
+            await_weights(held)
             if held < half_ring:
                 for copy in forward_copies(held + 1):
                     copy.start()
@@ -377,13 +389,14 @@
             at = pl.ds(p * channels, 2 * channels)
             mine[c][:, at] = pick(c, at) + step_size * pair_of
 
-    def edge_copy(dst, slot, to):
+    def edge_copy(slot, to):
         return pltpu.make_async_remote_copy(
-            src_ref=mine[0], dst_ref=dst, send_sem=edge_send.at[slot], recv_sem=edge_recv.at[slot],
+            src_ref=mine[0], dst_ref=around.at[slot], send_sem=edge_send.at[0],
+            recv_sem=edge_recv.at[0],
             device_id={"win": to}, device_id_type=MESH,
         )
 
-    edges = (edge_copy(before, 0, up_win), edge_copy(after, 1, down_win))
+    edges = (edge_copy(0, up_win), edge_copy(1, down_win))
 
     def blend():
         edge = 2 * FD
@@ -398,7 +411,7 @@
             own_w = jnp.where(hit, ramps_ref[2 * i, win], own_w)
             theirs_w = jnp.where(hit, ramps_ref[2 * i + 1, win], theirs_w)
         aligned = jnp.zeros((edge, wide), F32)
-        earlier, later = before[...], after[...]
+        earlier, later = around[0], around[1]
         for o in range(1, FD + 1):
             hit = first_half & ((zero + over_prev) == o)
             aligned = jnp.where(hit, pltpu.roll(earlier, o, 0), aligned)
@@ -420,8 +433,8 @@
         copy.start()
     gather_bin(1)
     gather_bin(2)
-    for copy in edges:
-        copy.wait()
+    await_bytes(around, edge_send.at[0])
+    await_bytes(around, edge_recv.at[0])
     blend()
     gather_bin(3)
     gather_bin(4)
@@ -431,14 +444,13 @@
     out_ref[: 2 * FD, :] = jnp.where(first_half, mine[0][...], turned)
     out_ref[frames - 2 * FD :, :] = jnp.where(first_half, turned, mine[0][...])
 
-    for t in range(3):
-        for slot in range(len(peers)):
-            await_bytes(kv.at[0, :, own_part, :], kv_send.at[t, slot])
+    await_bytes(kv.at[:, :, pl.ds(0, len(peers) * rows), :], kv_send.at[0])
+    await_bytes(kv.at[0, :, pl.ds(0, len(peers) * rows), :], kv_send.at[1])
     if ring:
         await_bytes(weights.at[:last], w_send.at[0])
     for c in range(2):
-        for send in (side_send, own_send, cross_send):
-            await_bytes(cross_in[c], send.at[c])
+        await_bytes(hidden[c], part_send.at[c, 0])
+        await_bytes(cross_in[c], part_send.at[c, 1])
 
 
 def local(
@@ -498,20 +510,18 @@
             both(lambda size: (n_blk, size, width), F32),
             both(lambda size: (size, 128), F32),
             (edge, pltpu.VMEM((frames - 2 * FD, wide), F32)),
-            edge, edge,
+            pltpu.VMEM((2, 2 * FD, wide), F32),
             pltpu.VMEM((16, channels), F32),
-            pltpu.VMEM((1, model), F32),
-            pltpu.VMEM((1, model), F32),
-            pltpu.VMEM((1, model), F32),
+            pltpu.VMEM((3, rows, features), BF16),
+            pltpu.VMEM((3, 1, model), F32),
             pltpu.VMEM((channels, model), head_weight.dtype),
             pltpu.VMEM((frames, wide), F32),
             pltpu.SMEM((1,), F32),
             pltpu.SMEM((n_win,), jnp.int32),
             pltpu.SMEM((2 * FD, n_win), jnp.int32),
-            dma((3, 3)), dma((heads,)), dma((1,)), dma((2, heads)), dma((2,)),
-            dma((1,)), dma((n_blk,)), dma((1,)), dma((3,)), dma((8,)),
-            dma((2,)), dma((2,)), dma((2,)), dma((2,)),
-            dma((2,)), dma((5,)), dma((2,)), dma((2,)),
+            dma((2,)), dma((2,)), dma((heads,)), dma((heads + 1,)), dma((2,)),
+            dma((1,)), dma((n_blk // 2,)), dma((1,)), dma((1,)), dma((6,)),
+            dma((2, 2)), dma((2,)), dma((2,)), dma((5,)), dma((1,)), dma((1,)),
         ],
         compiler_params=pltpu.CompilerParams(
             collective_id=0, has_side_effects=True, vmem_limit_bytes=60 * 1024 * 1024

time: 106 us -> 106 us (level)
  no operation moved by 1% of the time
where the time goes in v4:
time: 106 us
  Pallas kernels  104 us (98%)
    pallas_call x1, Pallas kernels, local(): pl.pallas_call(functools.partial(kernel, ring, n_blk), out_shape=pltpu.VM...  104 us

profile of v4, /device:TPU:0, one launch (start us, length us, event | category | flops | bytes accessed | tf_op | source)
XLA Modules:
  0.0 105.5 jit_solution(8621204560007908237)
XLA Ops:
  0.7 104.2 %shard_map.127 = f32[16,1024]{1,0:T(8,128)S(1)} custom-call(bf16[256,2560]{1,0:T(8,128)(2,1)} %q_ref.1, bf16[256,2560]{1,0:T(8,128)(2,1)} %k_ref.1, bf16[256,2560]{1,0:T(8,128)(2,1)} %v_ref.1, bf16[256,5120]{1,0:T(8,128)(2,1)} %stream_ref.1, bf16[640,640]{1,0:T(8,128)(2,1)} %ow_ref.1, f32[1,5120]{1,0:T(1,128)} %bitcast.8, f32[1,5120]{1,0:T(1,128)} %bitcast.9, ...), custom_call_target="tpu_custom_call" | custom-call | tf_op jit(solution)/shard_map/pallas_call | solution.py:497
  104.9 0.6 copy.15

commit v5 on v4

--- a/solution.py
+++ b/solution.py
@@ -324,6 +324,15 @@
     await_bytes(stream_ref, res_sem.at[0])
     await_bytes(weights.at[: 1 if ring else n_blk], w_local.at[0])
     held = 1
+
+    def advance():
+        nonlocal held
+        held += 1
+        await_weights(held)
+        if held < half_ring:
+            for copy in forward_copies(held + 1):
+                copy.start()
+
     for step in order:
         if step is None:
             far_rows = spots(far_chip, 2 * sizes[1])
@@ -332,12 +341,10 @@
             continue
         c, j = step
         if ring and (j + 1) // 2 > held:
-            held = (j + 1) // 2
-            await_weights(held)
-            if held < half_ring:
-                for copy in forward_copies(held + 1):
-                    copy.start()
+            advance()
         project(c, j)
+        if ring and step == steps[0]:
+            advance()
 
     state = [dict(raw=None, pivot=None, centres=[], spreads=[]) for _ in range(2)]
 

time: 106 us -> 105 us (level)
    pallas_call x1, Pallas kernels: 104 us -> 103 us  [local(): pl.pallas_call(functools.partial(kernel, ring, n_blk), out_shape=pltpu.VM...]
where the time goes in v5:
time: 105 us; the launch traced here: 104 us
  Pallas kernels  103 us (98%)
    pallas_call x1, Pallas kernels, local(): pl.pallas_call(functools.partial(kernel, ring, n_blk), out_shape=pltpu.VM...  103 us

profile of v5, /device:TPU:0, one launch (start us, length us, event | category | flops | bytes accessed | tf_op | source)
XLA Modules:
  0.0 104.4 jit_solution(11927034309779351311)
XLA Ops:
  0.7 103.1 %shard_map.127 = f32[16,1024]{1,0:T(8,128)S(1)} custom-call(bf16[256,2560]{1,0:T(8,128)(2,1)} %q_ref.1, bf16[256,2560]{1,0:T(8,128)(2,1)} %k_ref.1, bf16[256,2560]{1,0:T(8,128)(2,1)} %v_ref.1, bf16[256,5120]{1,0:T(8,128)(2,1)} %stream_ref.1, bf16[640,640]{1,0:T(8,128)(2,1)} %ow_ref.1, f32[1,5120]{1,0:T(1,128)} %bitcast.8, f32[1,5120]{1,0:T(1,128)} %bitcast.9, ...), custom_call_target="tpu_custom_call" | custom-call | tf_op jit(solution)/shard_map/pallas_call | solution.py:504
  103.8 0.6 copy.15

commit v6 on v5

--- a/solution.py
+++ b/solution.py
@@ -346,7 +346,7 @@
         if ring and step == steps[0]:
             advance()
 
-    state = [dict(raw=None, pivot=None, centres=[], spreads=[]) for _ in range(2)]
+    state = [dict(raw=None, pivot=None, seen=0) for _ in range(2)]
 
     def gather(c, j):
         now = state[c]
@@ -361,8 +361,15 @@
         now["raw"] = term if now["raw"] is None else now["raw"] + term
         centre = jnp.sum(shifted, axis=-1, keepdims=True) * (1.0 / width)
         centred = shifted - centre
-        now["centres"].append(centre)
-        now["spreads"].append(jnp.sum(centred * centred, axis=-1, keepdims=True))
+        spread = jnp.sum(centred * centred, axis=-1, keepdims=True)
+        seen = now["seen"]
+        if seen:
+            apart = centre - now["mean"]
+            now["mean"] += apart * (1.0 / (seen + 1))
+            now["spread"] += spread + apart * apart * (width * seen / (seen + 1))
+        else:
+            now["mean"], now["spread"] = centre, spread
+        now["seen"] = seen + 1
 
     step_size = step_ref[0]
     chunk_frames = (2 * FD, frames - 2 * FD)
@@ -379,10 +386,7 @@
 
     def freshen(c):
         now = state[c]
-        mean = functools.reduce(jnp.add, now["centres"]) * (1.0 / n_blk)
-        spread = functools.reduce(jnp.add, now["spreads"])
-        for centre in now["centres"]:
-            spread = spread + width * (centre - mean) * (centre - mean)
+        mean, spread = now["mean"], now["spread"]
         inverse = 1.0 / jnp.sqrt(spread * (1.0 / (width * n_blk)) + EPSILON)
         flat[c][:, :channels] = inverse * (now["raw"] - mean * head_rows[:1]) + head_rows[8:9]
         for p in range(0, per_frame, 2):

time: 105 us -> 105 us (level)
  no operation moved by 1% of the time
where the time goes in v6:
time: 105 us; the launch traced here: 104 us
  Pallas kernels  103 us (98%)
    pallas_call x1, Pallas kernels, local(): pl.pallas_call(functools.partial(kernel, ring, n_blk), out_shape=pltpu.VM...  103 us

profile of v6, /device:TPU:0, one launch (start us, length us, event | category | flops | bytes accessed | tf_op | source)
XLA Modules:
  0.0 104.3 jit_solution(1996318714275576426)
XLA Ops:
  0.7 103.0 %shard_map.127 = f32[16,1024]{1,0:T(8,128)S(1)} custom-call(bf16[256,2560]{1,0:T(8,128)(2,1)} %q_ref.1, bf16[256,2560]{1,0:T(8,128)(2,1)} %k_ref.1, bf16[256,2560]{1,0:T(8,128)(2,1)} %v_ref.1, bf16[256,5120]{1,0:T(8,128)(2,1)} %stream_ref.1, bf16[640,640]{1,0:T(8,128)(2,1)} %ow_ref.1, f32[1,5120]{1,0:T(1,128)} %bitcast.8, f32[1,5120]{1,0:T(1,128)} %bitcast.9, ...), custom_call_target="tpu_custom_call" | custom-call | tf_op jit(solution)/shard_map/pallas_call | solution.py:508
  103.7 0.6 copy.15

commit v7 on v6

--- a/solution.py
+++ b/solution.py
@@ -23,8 +23,8 @@
     kv, queries, attended, weights, residual, far_hold, near_hold, side_out, side_in, own_out,
     own_in, cross_out, cross_in, hidden, flat, mine, around, head_rows,
     staged, vectors, wt_ref, lat_ref, step_ref, inter_ref, ramps_ref, stage_sem,
-    kv_send, kv_recv, q_far, own_sem, w_send, w_recv, w_local, res_sem,
-    par_sem, part_send, side_recv, own_recv, cross_recv, edge_send,
+    kv_send, kv_recv, q_far, own_sem, w_send, w_recv,
+    part_send, side_recv, own_recv, cross_recv, edge_send,
     edge_recv,
 ):
     win, n_win = lax.axis_index("win"), lax.axis_size("win")
@@ -91,14 +91,14 @@
             src_ref=pair[t].at[:, head_columns(to, h)],
             dst_ref=kv.at[t, h, spots(me, rows), :],
             send_sem=kv_send.at[0],
-            recv_sem=kv_recv.at[h],
+            recv_sem=kv_recv.at[h // (heads - 1)],
             device_id={"fsdp": to},
             device_id_type=MESH,
         )
 
     def kv_own(t, h):
         return pltpu.make_async_copy(
-            pair[t].at[:, head_columns(me, h)], kv.at[t, h, spots(me, rows), :], own_sem.at[0]
+            pair[t].at[:, head_columns(me, h)], kv.at[t, h, spots(me, rows), :], stage_sem.at[0]
         )
 
     def q_copy(p, h, to, slot):
@@ -108,7 +108,7 @@
             src_ref=staged.at[2, pl.ds(first, length), head_columns(to, h)],
             dst_ref=queries[chunk].at[h, spots(me, sizes[chunk], start, length), :],
             send_sem=kv_send.at[1],
-            recv_sem=own_sem.at[1] if near else q_far.at[h if chunk == 0 else heads],
+            recv_sem=own_sem.at[0] if near else q_far.at[h if chunk == 0 else heads],
             device_id={"fsdp": to},
             device_id_type=MESH,
         )
@@ -118,7 +118,7 @@
         return pltpu.make_async_copy(
             staged.at[2, pl.ds(first, length), head_columns(me, h)],
             queries[chunk].at[h, spots(me, sizes[chunk], start, length), :],
-            own_sem.at[1],
+            own_sem.at[0],
         )
 
     def weight_copy(src, dst, slot, to):
@@ -150,30 +150,28 @@
 
     def weight_local(j):
         source = ow_ref if ring else ow_ref.at[:, columns(j)]
-        return pltpu.make_async_copy(source, weights.at[j], w_local.at[0])
+        return pltpu.make_async_copy(source, weights.at[j], stage_sem.at[1])
 
     def residual_copy(p):
         chunk, first, start, length = pieces[p]
         return pltpu.make_async_copy(
             stream_ref.at[pl.ds(first, length), :],
             residual[chunk].at[pl.ds(start, length), :],
-            res_sem.at[0],
+            stage_sem.at[1],
         )
 
     loads = [
-        pltpu.make_async_copy(src, vectors.at[i], par_sem.at[0])
+        pltpu.make_async_copy(src, vectors.at[i], stage_sem.at[1])
         for i, src in enumerate((scale_hbm, shift_hbm, gate_hbm))
     ]
     others = [
-        pltpu.make_async_copy(src, dst, par_sem.at[1 + i])
-        for i, (src, dst) in enumerate(
-            (
-                (wt_hbm, wt_ref),
-                (lat_hbm, lat_ref),
-                (step_hbm, step_ref),
-                (inter_hbm, inter_ref),
-                (ramps_hbm, ramps_ref),
-            )
+        pltpu.make_async_copy(src, dst, stage_sem.at[1])
+        for src, dst in (
+            (wt_hbm, wt_ref),
+            (lat_hbm, lat_ref),
+            (step_hbm, step_ref),
+            (inter_hbm, inter_ref),
+            (ramps_hbm, ramps_ref),
         )
     ]
 
@@ -217,16 +215,19 @@
             copy.start()
     lax.fori_loop(0, heads, functools.partial(start_q, chosen=(0, 1)), 0)
     lax.fori_loop(0, heads, functools.partial(start_q, chosen=(2,)), 0)
-    for copy in loads + others:
+    for copy in loads:
         copy.start()
+    await_bytes(vectors, stage_sem.at[1])
+    for copy in others:
+        copy.start()
+        copy.wait()
     for j in range(1 if ring else n_blk):
         weight_local(j).start()
+    await_bytes(weights.at[: 1 if ring else n_blk], stage_sem.at[1])
     for p in range(len(pieces)):
         residual_copy(p).start()
-
-    await_bytes(vectors, par_sem.at[0])
-    for copy in others:
-        copy.wait()
+    await_bytes(stream_ref, stage_sem.at[1])
+
     head = wt_ref[...].astype(F32)
     for i, vector in enumerate((scale_ref, shift_ref)):
         head_rows[8 * i : 8 * i + 8] = lax.dot_general(
@@ -249,7 +250,6 @@
         )
 
     def near_head(h, carry):
-        await_bytes(kv.at[:, h, pl.ds(0, len(peers) * rows), :], kv_recv.at[h])
         for c in range(2):
             attend(h, c, chip)
         return carry
@@ -261,13 +261,17 @@
         return carry
 
     own_part = pl.ds(0, rows)
+    await_bytes(kv.at[:, :, own_part, :], stage_sem.at[0])
     await_bytes(kv.at[:, :, own_part, :], own_sem.at[0])
-    await_bytes(kv.at[:, :, own_part, :], own_sem.at[1])
     if ring:
         await_weights(1)
         for copy in forward_copies(2):
             copy.start()
-    lax.fori_loop(0, heads, near_head, 0)
+    sent_part = pl.ds(0, len(peers) * rows)
+    await_bytes(kv.at[:, : heads - 1, sent_part, :], kv_recv.at[0])
+    lax.fori_loop(0, heads - 1, near_head, 0)
+    await_bytes(kv.at[:, heads - 1, sent_part, :], kv_recv.at[1])
+    near_head(heads - 1, 0)
     lax.fori_loop(0, heads, functools.partial(far_head, c=0), 0)
 
     if ring:
@@ -282,7 +286,8 @@
     turn = {step: i for i, step in enumerate(steps)}
     a_steps = [step for step in steps if step[0] == 0]
     b_steps = [step for step in steps if step[0] == 1]
-    bins = [a_steps, b_steps[:-3]] + [[step] for step in b_steps[-3:]]
+    bins = [a_steps, b_steps[:-2]] + [[step] for step in b_steps[-2:]]
+    cut = width - 128 if width > 128 else width
     bin_of = {step: i for i, several in enumerate(bins) for step in several}
 
     def part_copy(src, dst, send, recv, c, j, to):
@@ -297,8 +302,18 @@
     def own_copy(c, j):
         return part_copy(own_out, own_in, 0, own_recv.at[turn[c, j] % 2], c, j, sibling)
 
-    def cross_copy(c, j):
-        return part_copy(cross_out, cross_in, 1, cross_recv.at[bin_of[c, j]], c, j, far_sibling)
+    def cross_copies(c, j):
+        if (c, j) != steps[-1] or cut == width:
+            sem = cross_recv.at[bin_of[c, j]]
+            return [part_copy(cross_out, cross_in, 1, sem, c, j, far_sibling)]
+        return [
+            pltpu.make_async_remote_copy(
+                src_ref=cross_out[c].at[j, :, at], dst_ref=cross_in[c].at[j, :, at],
+                send_sem=part_send.at[c, 1], recv_sem=cross_recv.at[3 + i],
+                device_id={"fsdp": far_sibling}, device_id_type=MESH,
+            )
+            for i, at in enumerate((pl.ds(0, cut), pl.ds(cut, width - cut)))
+        ]
 
     def project(c, j):
         size = sizes[c]
@@ -315,14 +330,13 @@
         own_copy(c, j).start()
         side_copy(c, j).wait_recv()
         cross_out[c][j] = (far_hold[other_at, :] + side_in[c][j].astype(F32)).astype(BF16)
-        cross_copy(c, j).start()
+        for copy in cross_copies(c, j):
+            copy.start()
         own_copy(c, j).wait_recv()
         hidden[c][j] = residual[c][:, columns(j)].astype(F32) + gate_ref[:, columns(j)] * (
             near_hold[mine_at, :] + own_in[c][j].astype(F32)
         )
 
-    await_bytes(stream_ref, res_sem.at[0])
-    await_bytes(weights.at[: 1 if ring else n_blk], w_local.at[0])
     held = 1
 
     def advance():
@@ -348,28 +362,32 @@
 
     state = [dict(raw=None, pivot=None, seen=0) for _ in range(2)]
 
-    def gather(c, j):
+    def gather(c, j, low, high):
         now = state[c]
-        block = hidden[c][j] + gate_ref[:, columns(j)] * cross_in[c][j].astype(F32)
+        count = high - low
+        at = pl.ds(pl.multiple_of(blocks[j] * width + low, 128), count)
+        block = hidden[c][j, :, low:high] + gate_ref[:, at] * cross_in[c][j, :, low:high].astype(
+            F32
+        )
         if now["pivot"] is None:
-            now["pivot"] = jnp.sum(block, axis=-1, keepdims=True) * (1.0 / width)
+            now["pivot"] = jnp.sum(block, axis=-1, keepdims=True) * (1.0 / count)
         shifted = block - now["pivot"]
         term = lax.dot_general(
-            (shifted * scale_ref[:, columns(j)]).astype(BF16), wt_ref[:, columns(j)],
+            (shifted * scale_ref[:, at]).astype(BF16), wt_ref[:, at],
             (((1,), (1,)), ((), ())), preferred_element_type=F32,
         )
         now["raw"] = term if now["raw"] is None else now["raw"] + term
-        centre = jnp.sum(shifted, axis=-1, keepdims=True) * (1.0 / width)
+        centre = jnp.sum(shifted, axis=-1, keepdims=True) * (1.0 / count)
         centred = shifted - centre
         spread = jnp.sum(centred * centred, axis=-1, keepdims=True)
         seen = now["seen"]
         if seen:
             apart = centre - now["mean"]
-            now["mean"] += apart * (1.0 / (seen + 1))
-            now["spread"] += spread + apart * apart * (width * seen / (seen + 1))
+            now["mean"] += apart * (count / (seen + count))
+            now["spread"] += spread + apart * apart * (count * seen / (seen + count))
         else:
             now["mean"], now["spread"] = centre, spread
-        now["seen"] = seen + 1
+        now["seen"] = seen + count
 
     step_size = step_ref[0]
     chunk_frames = (2 * FD, frames - 2 * FD)
@@ -436,19 +454,23 @@
         c = bins[i][0][0]
         await_bytes(cross_in[c].at[: len(bins[i])], cross_recv.at[i])
         for step in bins[i]:
-            gather(*step)
+            gather(*step, 0, width)
 
     gather_bin(0)
     freshen(0)
     for copy in edges:
         copy.start()
     gather_bin(1)
-    gather_bin(2)
     await_bytes(around, edge_send.at[0])
     await_bytes(around, edge_recv.at[0])
     blend()
-    gather_bin(3)
-    gather_bin(4)
+    gather_bin(2)
+    if cut == width:
+        gather_bin(3)
+    else:
+        for i, (low, high) in enumerate(((0, cut), (cut, width))):
+            await_bytes(cross_in[1].at[steps[-1][1], :, low:high], cross_recv.at[3 + i])
+            gather(*steps[-1], low, high)
     freshen(1)
 
     turned = pltpu.roll(mine[1][...], FD, 0)
@@ -530,8 +552,8 @@
             pltpu.SMEM((1,), F32),
             pltpu.SMEM((n_win,), jnp.int32),
             pltpu.SMEM((2 * FD, n_win), jnp.int32),
-            dma((2,)), dma((2,)), dma((heads,)), dma((heads + 1,)), dma((2,)),
-            dma((1,)), dma((n_blk // 2,)), dma((1,)), dma((1,)), dma((6,)),
+            dma((2,)), dma((2,)), dma((2,)), dma((heads + 1,)), dma((1,)),
+            dma((1,)), dma((n_blk // 2,)),
             dma((2, 2)), dma((2,)), dma((2,)), dma((5,)), dma((1,)), dma((1,)),
         ],
         compiler_params=pltpu.CompilerParams(

time: 105 us -> 105 us (level)
  no operation moved by 1% of the time
where the time goes in v7:
time: 105 us; the launch traced here: 104 us
  Pallas kernels  103 us (98%)
    pallas_call x1, Pallas kernels, local(): pl.pallas_call(functools.partial(kernel, ring, n_blk), out_shape=pltpu.VM...  103 us

profile of v7, /device:TPU:0, one launch (start us, length us, event | category | flops | bytes accessed | tf_op | source)
XLA Modules:
  0.0 104.2 jit_solution(2180091706966417786)
XLA Ops:
  0.7 102.9 %shard_map.127 = f32[16,1024]{1,0:T(8,128)S(1)} custom-call(bf16[256,2560]{1,0:T(8,128)(2,1)} %q_ref.1, bf16[256,2560]{1,0:T(8,128)(2,1)} %k_ref.1, bf16[256,2560]{1,0:T(8,128)(2,1)} %v_ref.1, bf16[256,5120]{1,0:T(8,128)(2,1)} %stream_ref.1, bf16[640,640]{1,0:T(8,128)(2,1)} %ow_ref.1, f32[1,5120]{1,0:T(1,128)} %bitcast.8, f32[1,5120]{1,0:T(1,128)} %bitcast.9, ...), custom_call_target="tpu_custom_call" | custom-call | tf_op jit(solution)/shard_map/pallas_call | solution.py:530
  103.6 0.6 copy.15

commit v8 on v7

--- a/solution.py
+++ b/solution.py
@@ -394,14 +394,6 @@
     index = lax.broadcasted_iota(jnp.int32, (2 * FD, 1), 0)
     first_half = index < FD
 
-    def pick(c, at):
-        if c == 0:
-            return jnp.where(first_half, lat_ref[: 2 * FD, at], lat_ref[frames - 2 * FD :, at])
-        spread_over = pltpu.roll(
-            jnp.where(first_half, lat_ref[frames - 2 * FD :, at], lat_ref[: 2 * FD, at]), FD, 0
-        )
-        return spread_over
-
     def freshen(c):
         now = state[c]
         mean, spread = now["mean"], now["spread"]
@@ -416,11 +408,17 @@
                 axis=1,
             )
             at = pl.ds(p * channels, 2 * channels)
-            mine[c][:, at] = pick(c, at) + step_size * pair_of
+            if c == 0:
+                start = jnp.where(first_half, lat_ref[: 2 * FD, at], lat_ref[2 * FD :, at])
+                mine[:, at] = start + step_size * pair_of
+            else:
+                turned = pltpu.roll(step_size * pair_of, FD, 0)
+                out_ref[: 2 * FD, at] += jnp.where(first_half, 0.0, turned)
+                out_ref[2 * FD :, at] += jnp.where(first_half, turned, 0.0)
 
     def edge_copy(slot, to):
         return pltpu.make_async_remote_copy(
-            src_ref=mine[0], dst_ref=around.at[slot], send_sem=edge_send.at[0],
+            src_ref=mine, dst_ref=around.at[slot], send_sem=edge_send.at[0],
             recv_sem=edge_recv.at[0],
             device_id={"win": to}, device_id_type=MESH,
         )
@@ -448,7 +446,7 @@
             aligned = jnp.where(hit, pltpu.roll(later, edge - o, 0), aligned)
         theirs = theirs_w.astype(F32)
         own = jnp.where(own_w > 0, own_w, 1).astype(F32)
-        mine[0][...] = (theirs * aligned + own * mine[0][...]) / (theirs + own)
+        mine[...] = (theirs * aligned + own * mine[...]) / (theirs + own)
 
     def gather_bin(i):
         c = bins[i][0][0]
@@ -464,6 +462,8 @@
     await_bytes(around, edge_send.at[0])
     await_bytes(around, edge_recv.at[0])
     blend()
+    out_ref[: 2 * FD, :] = jnp.where(first_half, mine[...], lat_ref[: 2 * FD, :])
+    out_ref[2 * FD :, :] = jnp.where(first_half, lat_ref[2 * FD :, :], mine[...])
     gather_bin(2)
     if cut == width:
         gather_bin(3)
@@ -472,10 +472,6 @@
             await_bytes(cross_in[1].at[steps[-1][1], :, low:high], cross_recv.at[3 + i])
             gather(*steps[-1], low, high)
     freshen(1)
-
-    turned = pltpu.roll(mine[1][...], FD, 0)
-    out_ref[: 2 * FD, :] = jnp.where(first_half, mine[0][...], turned)
-    out_ref[frames - 2 * FD :, :] = jnp.where(first_half, turned, mine[0][...])
 
     await_bytes(kv.at[:, :, pl.ds(0, len(peers) * rows), :], kv_send.at[0])
     await_bytes(kv.at[0, :, pl.ds(0, len(peers) * rows), :], kv_send.at[1])
@@ -542,7 +538,7 @@
             parts, parts, parts, parts, parts, parts,
             both(lambda size: (n_blk, size, width), F32),
             both(lambda size: (size, 128), F32),
-            (edge, pltpu.VMEM((frames - 2 * FD, wide), F32)),
+            edge,
             pltpu.VMEM((2, 2 * FD, wide), F32),
             pltpu.VMEM((16, channels), F32),
             pltpu.VMEM((3, rows, features), BF16),

time: 105 us -> 105 us (level)
  no operation moved by 1% of the time
where the time goes in v8:
time: 105 us; the launch traced here: 104 us
  Pallas kernels  103 us (98%)
    pallas_call x1, Pallas kernels, local(): pl.pallas_call(functools.partial(kernel, ring, n_blk), out_shape=pltpu.VM...  103 us

profile of v8, /device:TPU:0, one launch (start us, length us, event | category | flops | bytes accessed | tf_op | source)
XLA Modules:
  0.0 104.2 jit_solution(3903427885903550705)
XLA Ops:
  0.7 102.9 %shard_map.127 = f32[16,1024]{1,0:T(8,128)S(1)} custom-call(bf16[256,2560]{1,0:T(8,128)(2,1)} %q_ref.1, bf16[256,2560]{1,0:T(8,128)(2,1)} %k_ref.1, bf16[256,2560]{1,0:T(8,128)(2,1)} %v_ref.1, bf16[256,5120]{1,0:T(8,128)(2,1)} %stream_ref.1, bf16[640,640]{1,0:T(8,128)(2,1)} %ow_ref.1, f32[1,5120]{1,0:T(1,128)} %bitcast.8, f32[1,5120]{1,0:T(1,128)} %bitcast.9, ...), custom_call_target="tpu_custom_call" | custom-call | tf_op jit(solution)/shard_map/pallas_call | solution.py:526
  103.6 0.6 copy.15
